TPU v7x, 256 devices: a whole 4x4x8 slice. The times are simulated.
256 devices in a mesh: blk: 128 (over x, z, y_hi, core), rep: 2 (over y_lo).
Axes of the slice: x: 4, y: 4 (y_hi: 2, y_lo: 2; y = y_hi * 2 + y_lo), z: 8, core: 2. Of those that a mesh axis runs over, the one named last changes fastest.
Arguments:
- frames: bfloat16 [2, 6144, 384], P('rep', 'blk'), may hold values from -600 to 600
- codebook: bfloat16 [131072, 384], P('blk'), may hold values from -2 to 2
Outputs:
- log_total: float32 [2, 6144], P('rep', 'blk')
- counts: float32 [131072], P('blk')
- entropy: float32 [], replicated
All inputs are finite; a program needn't handle non-finite values.
Results may differ from a plain program's by a relative error of at most 0.00065.
Values may be sent and summed in bfloat16 or wider, within the bound.
No kernel may reach another device: no remote copies, remote signals or barrier semaphores. Data moves between devices by JAX's collectives and lax.ppermute only.
A program may use at most 128 MiB of HBM per device.

v0:
```python
import functools

import jax
import jax.numpy as jnp
from jax import lax
from jax.sharding import Mesh
from jax.sharding import PartitionSpec as P

BLK = ("blk_0", "blk_1", "blk_2", "blk_3")


def gathered_once(array, axis):
    leaves = jax.tree.leaves(array)
    sequence = sorted(range(len(leaves)), key=lambda k: -leaves[k].size)
    width = (1, *leaves[sequence[0]].shape)[-1]
    lines = [
        jnp.pad(leaves[k].reshape(-1), (0, -leaves[k].size % width)).reshape(-1, width)
        for k in sequence
    ]
    both, at, found = (lax.all_gather(jnp.concatenate(lines), axis), 0, {})
    for k, line in zip(sequence, lines):
        slab = both[:, at : at + len(line)].reshape(len(both), -1)
        found[k] = slab[:, : leaves[k].size].reshape(-1, *leaves[k].shape)
        at += len(line)
    numbers = iter(range(len(leaves)))
    return jax.tree.map(lambda _: found[next(numbers)], array)


def merged_by_axis(array, axes, combine):
    for axis in axes:
        pieces = gathered_once(array, axis)
        array = jax.tree.map(lambda part: part[0], pieces)
        for k in range(1, lax.axis_size(axis)):
            array = combine(array, jax.tree.map(lambda part: part[k], pieces))
    return array


def from_everyone(array, axis):
    copies = jnp.broadcast_to(array, (lax.axis_size(axis), *array.shape))
    return lax.all_to_all(copies, axis, split_axis=0, concat_axis=0, tiled=True)


def taken_together(array, axis):
    everything = from_everyone(array, axis)
    return jnp.sum(everything, axis=0)


def one_axis_at_a_time(array, axes):
    return functools.reduce(lax.psum, axes, array)


def score_block(moving, codebook):
    return lax.dot_general(
        moving, codebook, (((1,), (1,)), ((), ())), preferred_element_type=jnp.float32
    )


def merge_stats(earlier, later):
    new_high = jnp.maximum(earlier[0], later[0])
    new_total = earlier[1] * jnp.exp(earlier[0] - new_high) + later[1] * jnp.exp(
        later[0] - new_high
    )
    return (new_high, new_total)


def entropy_part(usage, frames_total):
    mean_use = usage / frames_total
    return -jnp.sum(mean_use * jnp.log(mean_use + 1e-07))


def per_device(frames, codebook):
    frame_rows = frames[0]
    shard_rows = frame_rows.shape[0]
    cycle_size = lax.axis_size(BLK)
    cycle_index = lax.axis_index(BLK)
    group_rows = shard_rows * cycle_size
    scores = score_block(lax.all_gather(frame_rows, BLK, axis=0, tiled=True), codebook)
    local_high = jnp.max(scores, axis=1)
    local_total = jnp.sum(jnp.exp(scores - local_high[:, None]), axis=1)
    row_high, row_total = merged_by_axis((local_high, local_total), BLK, merge_stats)
    lse_all = row_high + jnp.log(row_total)
    lse_own = lax.dynamic_slice_in_dim(lse_all, cycle_index * shard_rows, shard_rows, 0)
    usage_part = jnp.sum(jnp.exp(scores - lse_all[:, None]), axis=0)
    frames_total = group_rows * lax.axis_size("rep")
    usage = taken_together(usage_part, "rep")
    entropy = one_axis_at_a_time(entropy_part(usage, frames_total), BLK)
    return (lse_own[None, :], usage, entropy)


def solution(mesh):
    split = Mesh(
        mesh.devices.reshape(4, 8, 2, 2, mesh.shape["rep"]),
        ("blk_0", "blk_1", "blk_2", "blk_3", "rep"),
    )
    return jax.shard_map(
        per_device,
        mesh=split,
        in_specs=(P("rep", BLK, None), P(BLK, None)),
        out_specs=(P("rep", BLK), P(BLK), P()),
        check_vma=False,
    )
```

profile of v0, /device:TPU:1, one launch (start us, length us, event | category | flops | bytes accessed | tf_op | source)
XLA Modules:
  0.0 265.5 jit_solution(1867115252379620708)
XLA Ops:
  7.2 0.0 copy-start
  7.2 0.0 all-gather.11.cloned.1.call-start
  7.2 0.7 all-gather.11.cloned.1.call-update
  7.9 128.6 %all-gather.11.cloned.1.call-done = bf16[1,6144,384]{2,1,0:T(8,128)(2,1)} async-done(((bf16[1,48,384]{2,1,0:T(8,128)(2,1)}), bf16[1,6144,384]{2,1,0:T(8,128)(2,1)}) %all-gather.11.cloned.1.call-update) | async-done | bytes 4718608 | tf_op jit(solution)/shard_map/all_gather | solution.py:77
  136.5 0.0 copy-done
  136.5 14.0 %fusion.52 = (f32[6144]{0:T(1024)S(1)}, f32[6144,1024]{0,1:T(8,128)}) fusion(bf16[1024,384]{1,0:T(8,128)(2,1)S(1)} %copy-done, bf16[1,6144,384]{2,1,0:T(8,128)(2,1)} %all-gather.11.cloned.1.call-done), kind=kOutput, calls=%fused_computation.87 | convolution fusion | flops 4838123520 | bytes 30695424 | tf_op jit(solution)/shard_map/dot_general | solution.py:53
  150.5 0.0 copy-start.1
  150.5 10.4 %exponential_reduce_fusion.1 = f32[6144]{0:T(1024)S(1)} fusion(f32[6144,1024]{0,1:T(8,128)} %get-tuple-element.14, f32[6144]{0:T(1024)S(1)} %get-tuple-element.13), kind=kLoop, calls=%fused_computation.1 | loop fusion | flops 12576768 | bytes 25214976 | tf_op jit(solution)/shard_map/reduce_sum | solution.py:79
  161.0 10.2 %all-gather.5 = f32[4,2,6144]{2,1,0:T(2,128)S(1)} all-gather(f32[1,2,6144]{2,1,0:T(2,128)S(1)} %maximum_bitcast_fusion), channel_id=3, replica_groups=mesh['blk_0'=4,'blk_1'=8,'blk_2'=2,'blk_3'=2,'rep'=2] {'blk_0'}, dimensions={0}, use_global_device_ids=true | all-gather | bytes 245760 | tf_op jit(solution)/shard_map/all_gather | solution.py:20
  171.1 0.2 fusion.27
  171.4 19.0 %all-gather.6 = f32[8,2,6144]{2,1,0:T(2,128)S(1)} all-gather(f32[1,2,6144]{2,1,0:T(2,128)S(1)} %maximum_bitcast_fusion.1), channel_id=4, replica_groups=mesh['blk_0'=4,'blk_1'=8,'blk_2'=2,'blk_3'=2,'rep'=2] {'blk_1'}, dimensions={0}, use_global_device_ids=true | all-gather | bytes 442368 | tf_op jit(solution)/shard_map/all_gather | solution.py:20
  190.5 0.6 fusion.6
  191.1 5.1 %all-gather.7 = f32[2,2,6144]{2,1,0:T(2,128)S(1)} all-gather(f32[1,2,6144]{2,1,0:T(2,128)S(1)} %maximum_bitcast_fusion.2), channel_id=5, replica_groups=mesh['blk_0'=4,'blk_1'=8,'blk_2'=2,'blk_3'=2,'rep'=2] {'blk_2'}, dimensions={0}, use_global_device_ids=true | all-gather | bytes 147456 | tf_op jit(solution)/shard_map/all_gather | solution.py:20
  196.2 0.1 fusion.3
  196.4 11.4 %all-gather.8 = f32[2,2,6144]{2,1,0:T(2,128)S(1)} all-gather(f32[1,2,6144]{2,1,0:T(2,128)S(1)} %maximum_bitcast_fusion.3), channel_id=6, replica_groups=mesh['blk_0'=4,'blk_1'=8,'blk_2'=2,'blk_3'=2,'rep'=2] {'blk_3'}, dimensions={0}, use_global_device_ids=true | all-gather | bytes 147456 | tf_op jit(solution)/shard_map/all_gather | solution.py:20
  207.8 0.1 fusion.51
  207.9 0.0 copy-done.1
  207.9 3.8 %exponential_reduce_fusion = f32[1024]{0:T(1024)S(1)} fusion(f32[6144,1024]{0,1:T(8,128)S(1)} %copy-done.1, f32[6144]{0:T(1024)S(1)} %log_add_fusion), kind=kLoop, calls=%fused_computation | loop fusion | flops 12581888 | bytes 25194496 | tf_op jit(solution)/shard_map/reduce_sum | solution.py:83
  211.7 0.6 broadcast_in_dim.9
  212.3 3.2 %all-to-all-start = ((f32[2,1,1024]{2,1,0:T(1,128)}), f32[2,1,1024]{2,1,0:T(1,128)S(1)}, u32[]{:S(2)}, u32[]{:S(2)}) async-start(f32[2,1,1024]{2,1,0:T(1,128)} %broadcast_in_dim.9), calls=%async_computation | async-start | bytes 16384 | tf_op jit(solution)/shard_map/all_to_all | solution.py:40
  215.6 2.6 all-to-all-done
  218.2 0.0 copy-start.2
  218.3 0.6 multiply_reduce_fusion
  219.5 8.9 %psum.28 = f32[]{:T(128)} all-reduce(f32[]{:T(128)S(6)} %neg.3), channel_id=1, replica_groups=mesh['blk_0'=4,'blk_1'=8,'blk_2'=2,'blk_3'=2,'rep'=2] {'blk_0'}, use_global_device_ids=true, to_apply=%region_5.6 | all-reduce | flops 1 | bytes 8 | tf_op jit(solution)/shard_map/psum | solution.py:49
  228.5 12.5 %psum.29 = f32[]{:T(128)} all-reduce(f32[]{:T(128)} %psum.28), channel_id=1, replica_groups=mesh['blk_0'=4,'blk_1'=8,'blk_2'=2,'blk_3'=2,'rep'=2] {'blk_1'}, use_global_device_ids=true, to_apply=%region_6.7 | all-reduce | flops 1 | bytes 8 | tf_op jit(solution)/shard_map/psum | solution.py:49
  241.0 5.9 %psum.30 = f32[]{:T(128)} all-reduce(f32[]{:T(128)} %psum.29), channel_id=1, replica_groups=mesh['blk_0'=4,'blk_1'=8,'blk_2'=2,'blk_3'=2,'rep'=2] {'blk_2'}, use_global_device_ids=true, to_apply=%region_7.8 | all-reduce | flops 1 | bytes 8 | tf_op jit(solution)/shard_map/psum | solution.py:49
  246.9 0.6 dynamic-slice_bitcast_fusion
  247.5 11.2 %psum.31 = f32[]{:T(128)} all-reduce(f32[]{:T(128)} %psum.30), channel_id=1, replica_groups=mesh['blk_0'=4,'blk_1'=8,'blk_2'=2,'blk_3'=2,'rep'=2] {'blk_3'}, use_global_device_ids=true, to_apply=%region_8.9 | all-reduce | flops 1 | bytes 8 | tf_op jit(solution)/shard_map/psum | solution.py:49
  258.6 0.0 copy-done.2
  (6 shorter events, 0.2 us)
Async XLA Ops:
  7.2 129.3 %copy-start = (bf16[1024,384]{1,0:T(8,128)(2,1)S(1)}, bf16[1024,384]{1,0:T(8,128)(2,1)}, u32[]{:S(2)}) copy-start(bf16[1024,384]{1,0:T(8,128)(2,1)} %param.3) | copy-start | bytes 2359300
  7.2 129.3 %all-gather.11.cloned.1.call-start = ((), (), s32[]{:S(2)}) async-start(), calls=%async_computation.1 | async-start | bytes 4755456 | tf_op jit(solution)/shard_map/all_gather | solution.py:77
  150.5 57.4 %copy-start.1 = (f32[6144,1024]{0,1:T(8,128)S(1)}, f32[6144,1024]{0,1:T(8,128)}, u32[]{:S(2)}) copy-start(f32[6144,1024]{0,1:T(8,128)} %get-tuple-element.14) | copy-start | bytes 75497472
  212.3 5.9 %all-to-all-start = ((f32[2,1,1024]{2,1,0:T(1,128)}), f32[2,1,1024]{2,1,0:T(1,128)S(1)}, u32[]{:S(2)}, u32[]{:S(2)}) async-start(f32[2,1,1024]{2,1,0:T(1,128)} %broadcast_in_dim.9), calls=%async_computation | async-start | bytes 16384 | tf_op jit(solution)/shard_map/all_to_all | solution.py:40
  218.2 40.4 %copy-start.2 = (f32[1024]{0:T(1024)}, f32[1024]{0:T(1024)S(1)}, u32[]{:S(2)}) copy-start(f32[1024]{0:T(1024)S(1)} %reduce_sum.38) | copy-start | bytes 12292
Sparse Core Ops, SparseCore 0:
  11.9 124.5 all-gather.10
where the time goes:
time: 266 us; the launch traced here: 265 us
  waiting for transfers between devices  132 us (50%)
  blocking collectives  84.3 us (32%)
  other arithmetic  16 us (6%)
  between operations  14.8 us (6%)
  matrix products  14 us (5%)
  starting transfers between devices  3.26 us (1%)
    all_gather x1, waiting for transfers between devices, per_device(): lax.all_gather(frame_rows, BLK, axis=0, tiled=True)  129 us
    all_gather x4, blocking collectives, gathered_once(): both, at, found = (lax.all_gather(jnp.concatenate(lines), axis), 0, {})  45.7 us
    psum x4, blocking collectives, one_axis_at_a_time(): return functools.reduce(lax.psum, axes, array)  38.5 us
    dot_general x1, matrix products, score_block(): lax.dot_general(moving, codebook, (((1,), (1,)), ((), ())), preferred_ele...  14 us
    reduce_sum x1, other arithmetic, per_device(): local_total = jnp.sum(jnp.exp(scores - local_high[:, None]), axis=1)  10.4 us
  transfers between devices with their start and end apart: 2, of which 2 were waited for; matrix products, arithmetic and copies ran while one was open for 0% of the time, Pallas kernels for 0%

commit v1 on v0

v1 whole, which is shorter than its diff:
```python
import functools

import jax
import jax.numpy as jnp
from jax import lax
from jax.experimental import pallas as pl
from jax.experimental.pallas import tpu as pltpu
from jax.sharding import Mesh
from jax.sharding import PartitionSpec as P

BLK = ("x", "z", "yh", "core")
RING_Y = ("yh", "rep")
COLUMN = ("yh", "core", "rep")
PLANE = ("x", "z")
LOG2E = 1.4426950408889634
VB = 256
FB = 256


def spread(array, axis):
    n = lax.axis_size(axis)
    copies = jnp.broadcast_to(array, (n, *array.shape))
    return lax.all_to_all(copies, axis, split_axis=0, concat_axis=0, tiled=True)


def tile_kernel(frames_ref, codes_ref, probs_ref, high_ref, total_ref):
    blocks = codes_ref.shape[0] // VB

    def scores_of(k):
        return lax.dot_general(
            codes_ref[pl.ds(k * VB, VB), :],
            frames_ref[...],
            (((1,), (1,)), ((), ())),
            preferred_element_type=jnp.float32,
        )

    for k in range(blocks):
        s = scores_of(k)
        high = jnp.max(s, axis=0, keepdims=True)
        p = jnp.exp2((s - high) * LOG2E)
        probs_ref[pl.ds(k * VB, VB), :] = p
        high_ref[pl.ds(k, 1), :] = high
        total_ref[pl.ds(k, 1), :] = jnp.sum(p, axis=0, keepdims=True)


def tile_stats(frames, codes):
    rows, width = frames.shape
    protos = codes.shape[0]
    blocks = protos // VB
    return pl.pallas_call(
        tile_kernel,
        grid=(rows // FB,),
        in_specs=[
            pl.BlockSpec((FB, width), lambda i: (i, 0)),
            pl.BlockSpec((protos, width), lambda i: (0, 0)),
        ],
        out_specs=[
            pl.BlockSpec((protos, FB), lambda i: (0, i)),
            pl.BlockSpec((blocks, FB), lambda i: (0, i)),
            pl.BlockSpec((blocks, FB), lambda i: (0, i)),
        ],
        out_shape=[
            jax.ShapeDtypeStruct((protos, rows), jnp.float32),
            jax.ShapeDtypeStruct((blocks, rows), jnp.float32),
            jax.ShapeDtypeStruct((blocks, rows), jnp.float32),
        ],
        compiler_params=pltpu.CompilerParams(
            dimension_semantics=("arbitrary",), vmem_limit_bytes=24 * 1024 * 1024
        ),
        cost_estimate=pl.CostEstimate(
            flops=2 * rows * protos * width,
            bytes_accessed=4 * rows * protos + 2 * (rows + protos) * width,
            transcendentals=rows * protos,
        ),
        name="tile_stats",
    )(frames, codes)


def absolute_order(parts, yh, core):
    parts = jnp.where(yh == 1, parts[::-1], parts)
    return jnp.where(core == 1, parts[:, ::-1], parts)


def per_device(frames, codebook):
    own = frames[0]
    shard_rows, width = own.shape
    owned = codebook.shape[0]
    yh, core = lax.axis_index("yh"), lax.axis_index("core")

    opposite = lax.ppermute(codebook, RING_Y, [(0, 3), (3, 0), (1, 2), (2, 1)])
    both = jnp.concatenate([codebook, opposite])
    swapped = lax.ppermute(both, "core", [(0, 1), (1, 0)])
    codes = jnp.stack(
        [codebook, swapped[:owned], opposite, swapped[owned:]]
    ).reshape(-1, width)

    line = spread(own, "z").reshape(-1, width)
    rows = spread(line, "x").reshape(-1, width)

    probs, high, total = tile_stats(rows, codes)
    top = jnp.max(high, axis=0)
    part_lse = top + jnp.log(jnp.sum(total * jnp.exp(high - top), axis=0))
    parts = spread(part_lse, PLANE)
    peak = jnp.max(parts, axis=0)
    lse = peak + jnp.log(jnp.sum(jnp.exp(parts - peak), axis=0))

    weight = jnp.exp(high - lse)
    blocks = weight.shape[0]
    usage = jnp.sum(
        probs.reshape(blocks, VB, -1) * weight[:, None, :], axis=2
    ).reshape(2, 2, owned)
    usage = absolute_order(usage, yh, core).reshape(-1)
    column = jnp.sum(spread(usage, COLUMN), axis=0)

    at = (lax.axis_index(PLANE)) * shard_rows
    lse_own = lax.dynamic_slice_in_dim(lse, at, shard_rows, 0)
    usage_own = lax.dynamic_slice_in_dim(column, (2 * yh + core) * owned, owned, 0)

    embeddings = shard_rows * lax.axis_size(BLK) * lax.axis_size("rep")
    mean_use = column / embeddings
    term = -jnp.sum(mean_use * jnp.log(mean_use + 1e-07), keepdims=True)
    entropy = jnp.sum(spread(term, PLANE))
    return (lse_own[None, :], usage_own, entropy)


def solution(mesh):
    split = Mesh(
        mesh.devices.reshape(4, 8, 2, 2, mesh.shape["rep"]),
        ("x", "z", "yh", "core", "rep"),
    )
    return jax.shard_map(
        per_device,
        mesh=split,
        in_specs=(P("rep", BLK, None), P(BLK, None)),
        out_specs=(P("rep", BLK), P(BLK), P()),
        check_vma=False,
    )
```

time: 266 us -> 142 us (0.53)
  waiting for transfers between devices: 132 us -> 51.5 us
  blocking collectives: 84.3 us -> 20.7 us
  starting transfers between devices: 3.26 us -> 25.1 us
  matrix products: 14 us -> 0 us
  Pallas kernels: 0 us -> 13.7 us
  between operations: 14.8 us -> 1.46 us
  local copies, waits for them, and re-layouts: 1.28 us -> 14.1 us
    all_gather x1 -> x0, waiting for transfers between devices: 129 us -> none  [per_device(): lax.all_gather(frame_rows, BLK, axis=0, tiled=True)]
    all_gather x4 -> x0, blocking collectives: 45.7 us -> none  [gathered_once(): both, at, found = (lax.all_gather(jnp.concatenate(lines), axis), 0, {})]
    psum x4 -> x0, blocking collectives: 38.5 us -> none  [one_axis_at_a_time(): return functools.reduce(lax.psum, axes, array)]
    all_to_all x1 -> x4, waiting for transfers between devices: 2.64 us -> 35 us  [spread(): return lax.all_to_all(copies, axis, split_axis=0, concat_axis=0, tiled=True)]
    all_to_all x0 -> x1, blocking collectives: none -> 20.7 us  [spread(): return lax.all_to_all(copies, axis, split_axis=0, concat_axis=0, tiled=True)]
    ppermute x0 -> x2, waiting for transfers between devices: none -> 16.5 us  [the longest x1 16.5 us: per_device(): opposite = lax.ppermute(codebook, RING_Y, [(0, 3), (3, 0), (1, 2), (2, 1)])]
    all_to_all x1 -> x4, starting transfers between devices: 3.22 us -> 19.3 us  [spread(): return lax.all_to_all(copies, axis, split_axis=0, concat_axis=0, tiled=True)]
    dot_general x1 -> x0, matrix products: 14 us -> none  [score_block(): lax.dot_general(moving, codebook, (((1,), (1,)), ((), ())), preferred_ele...]
  transfers between devices with their start and end apart: 2 -> 6, of which waited for: 2 -> 5; matrix products, arithmetic and copies ran while one was open for 0% -> 3% of each run, Pallas kernels for 0% -> 0%
where the time goes in v1:
time: 142 us
  waiting for transfers between devices  51.5 us (36%)
  starting transfers between devices  25.1 us (18%)
  blocking collectives  20.7 us (15%)
  other arithmetic  15.3 us (11%)
  local copies, waits for them, and re-layouts  14.1 us (10%)
  Pallas kernels  13.7 us (10%)
  between operations  1.46 us (1%)
    all_to_all x4, waiting for transfers between devices, spread(): return lax.all_to_all(copies, axis, split_axis=0, concat_axis=0, tiled=True)  35 us
    all_to_all x1, blocking collectives, spread(): return lax.all_to_all(copies, axis, split_axis=0, concat_axis=0, tiled=True)  20.7 us
    all_to_all x4, starting transfers between devices, spread(): return lax.all_to_all(copies, axis, split_axis=0, concat_axis=0, tiled=True)  19.3 us
    ppermute x1, waiting for transfers between devices, per_device(): opposite = lax.ppermute(codebook, RING_Y, [(0, 3), (3, 0), (1, 2), (2, 1)])  16.5 us
    pallas_call x1, Pallas kernels, tile_stats(): pl.pallas_call(tile_kernel, grid=(rows // FB,), in_specs=[pl.BlockSpec((F...  13.7 us
    reduce_sum x1, other arithmetic, per_device(): jnp.sum(probs.reshape(blocks, VB, -1) * weight[:, None, :], axis=2)  9.46 us
    unnamed x9, local copies, waits for them, and re-layouts  9.25 us
    ppermute x1, starting transfers between devices, per_device(): opposite = lax.ppermute(codebook, RING_Y, [(0, 3), (3, 0), (1, 2), (2, 1)])  3.64 us
  transfers between devices with their start and end apart: 6, of which 5 were waited for; matrix products, arithmetic and copies ran while one was open for 3% of the time, Pallas kernels for 0%

profile of v1, /device:TPU:1, one launch (start us, length us, event | category | flops | bytes accessed | tf_op | source)
XLA Modules:
  0.0 141.9 jit_solution(3289558962556472227)
XLA Ops:
  0.6 0.0 copy-start.3
  0.6 3.6 %collective-permute-start = (bf16[1024,384]{1,0:T(8,128)(2,1)}, bf16[1024,384]{1,0:T(8,128)(2,1)S(1)}, u32[]{:S(2)}, u32[]{:S(2)}) collective-permute-start(bf16[1024,384]{1,0:T(8,128)(2,1)} %param.3), channel_id=1, source_target_pairs={{0,5},{5,0},{1,4},{4,1},{2,7},{7,2},{3,6},{6,3},{8,13},{13,8},{9,1... | collective-permute-start | bytes 2359304 | tf_op jit(solution)/shard_map/ppermute | solution.py:90
  4.3 16.5 %collective-permute-done = bf16[1024,384]{1,0:T(8,128)(2,1)S(1)} collective-permute-done((bf16[1024,384]{1,0:T(8,128)(2,1)}, bf16[1024,384]{1,0:T(8,128)(2,1)S(1)}, u32[]{:S(2)}, u32[]{:S(2)}) %collective-permute-start) | collective-permute-done | bytes 786464 | tf_op jit(solution)/shard_map/ppermute | solution.py:90
  20.8 0.0 copy-start.1
  20.8 2.7 %pad_maximum_fusion.1 = bf16[2048,384]{1,0:T(8,128)(2,1)} fusion(bf16[1024,384]{1,0:T(8,128)(2,1)S(1)} %collective-permute-done, bf16[1024,384]{1,0:T(8,128)(2,1)} %param.3), kind=kLoop, calls=%fused_computation.3 | loop fusion | flops 3145728 | bytes 3145728 | tf_op jit(solution)/shard_map/concatenate | solution.py:91
  23.6 2.2 %collective-permute-start.1 = (bf16[2048,384]{1,0:T(8,128)(2,1)}, bf16[2048,384]{1,0:T(8,128)(2,1)S(1)}, u32[]{:S(2)}, u32[]{:S(2)}) collective-permute-start(bf16[2048,384]{1,0:T(8,128)(2,1)} %pad_maximum_fusion.1), channel_id=1, source_target_pairs={{0,2},{2,0},{1,3},{3,1},{4,6},{6,4},{5,7},{7,5},{8,10},{10,8},{9,1... | collective-permute-start | bytes 4718600 | tf_op jit(solution)/shard_map/ppermute | solution.py:92
  25.7 0.0 copy-done.3
  25.8 20.7 %all_to_all.31 = bf16[8,48,384]{2,1,0:T(8,128)(2,1)S(1)} all-to-all(bf16[8,48,384]{2,1,0:T(8,128)(2,1)S(1)} %broadcast_in_dim.25), channel_id=1, replica_groups=mesh['x'=4,'z'=8,'yh'=2,'core'=2,'rep'=2] {'z'}, dimensions={0} | all-to-all | bytes 589824 | tf_op jit(solution)/shard_map/all_to_all | solution.py:23
  46.4 1.1 broadcast_in_dim.26
  47.6 0.0 copy-done.1
  47.6 4.3 %all-to-all-start.1 = ((bf16[4,384,384]{2,1,0:T(8,128)(2,1)}), bf16[4,384,384]{2,1,0:T(8,128)(2,1)}, u32[]{:S(2)}, u32[]{:S(2)}) async-start(bf16[4,384,384]{2,1,0:T(8,128)(2,1)} %broadcast_in_dim.26), calls=%async_computation.1 | async-start | bytes 2359296 | tf_op jit(solution)/shard_map/all_to_all | solution.py:23
  51.8 0.0 copy-start.2
  51.8 0.0 collective-permute-done.1
  51.9 0.2 slice_bitcast_fusion.1
  52.0 0.9 copy-done.2
  53.0 1.5 %pad_maximum_fusion = bf16[4,1024,384]{2,1,0:T(8,128)(2,1)S(1)} fusion(bf16[1,1024,384]{2,1,0:T(8,128)(2,1)S(1)} %get-tuple-element.10, bf16[1,1024,384]{2,1,0:T(8,128)(2,1)S(1)} %bitcast.27, bf16[1,1024,384]{2,1,0:T(8,128)(2,1)S(1)} %get-tuple-element.9, bf16[1,1024,384]{2,1,0:T(8,128)(2,1)} %bitcast.26), kind=kLoop, calls=%fused_computation.2 | loop fusion | flops 4718592 | bytes 6291456 | tf_op jit(solution)/shard_map/stack | solution.py:93
  54.5 13.1 %all-to-all-done.1 = bf16[4,384,384]{2,1,0:T(8,128)(2,1)} async-done(((bf16[4,384,384]{2,1,0:T(8,128)(2,1)}), bf16[4,384,384]{2,1,0:T(8,128)(2,1)}, u32[]{:S(2)}, u32[]{:S(2)}) %all-to-all-start.1) | async-done | bytes 1179680 | tf_op jit(solution)/shard_map/all_to_all | solution.py:23
  67.6 13.7 %tile_stats.1 = (f32[4096,1536]{1,0:T(8,128)S(1)}, f32[16,1536]{1,0:T(8,128)S(1)}, f32[16,1536]{1,0:T(8,128)S(1)}) custom-call(bf16[1536,384]{1,0:T(8,128)(2,1)} %bitcast.2.frames_ref, bf16[4096,384]{1,0:T(8,128)(2,1)S(1)} %bitcast.25), custom_call_target="tpu_custom_call" | custom-call | flops 4831838208 | bytes 29491200 | tf_op jit(solution)/shard_map/tile_stats/pallas_call | solution.py:50
  81.3 0.0 copy-start
  81.3 8.3 %copy-done = f32[4096,1536]{1,0:T(8,128)} copy-done((f32[4096,1536]{1,0:T(8,128)}, f32[4096,1536]{1,0:T(8,128)S(1)}, u32[]{:S(2)}) %copy-start) | copy-done | bytes 25165848
  89.6 0.8 broadcast_in_dim.27
  90.4 3.9 %all-to-all-start.2 = ((f32[32,1,1536]{2,1,0:T(1,128)}), f32[32,1,1536]{2,1,0:T(1,128)S(1)}, u32[]{:S(2)}, u32[]{:S(2)}) async-start(f32[32,1,1536]{2,1,0:T(1,128)} %broadcast_in_dim.27), calls=%async_computation.2 | async-start | bytes 393216 | tf_op jit(solution)/shard_map/all_to_all | solution.py:23
  94.3 9.4 %all-to-all-done.2 = f32[32,1,1536]{2,1,0:T(1,128)S(1)} async-done(((f32[32,1,1536]{2,1,0:T(1,128)}), f32[32,1,1536]{2,1,0:T(1,128)S(1)}, u32[]{:S(2)}, u32[]{:S(2)}) %all-to-all-start.2) | async-done | bytes 196640 | tf_op jit(solution)/shard_map/all_to_all | solution.py:23
  103.7 0.1 reduce_max.19
  103.9 9.5 %fusion = f32[4096]{0:T(1024)S(1)} fusion(f32[4096,1536]{1,0:T(8,128)} %copy-done, f32[16,1536]{1,0:T(8,128)S(1)} %subtract_exponential_fusion), kind=kLoop, calls=%fused_computation.1 | loop fusion | flops 12578816 | bytes 25280512 | tf_op jit(solution)/shard_map/reduce_sum | solution.py:109
  113.4 0.2 rev.7
  113.7 0.7 broadcast_in_dim.30
  114.4 7.3 %all-to-all-start.3 = ((f32[8,1,4096]{2,1,0:T(1,128)}), f32[8,1,4096]{2,1,0:T(1,128)S(1)}, u32[]{:S(2)}, u32[]{:S(2)}) async-start(f32[8,1,4096]{2,1,0:T(1,128)} %broadcast_in_dim.30), calls=%async_computation.3 | async-start | bytes 262144 | tf_op jit(solution)/shard_map/all_to_all | solution.py:23
  121.7 5.1 %all-to-all-done.3 = f32[8,1,4096]{2,1,0:T(1,128)S(1)} async-done(((f32[8,1,4096]{2,1,0:T(1,128)}), f32[8,1,4096]{2,1,0:T(1,128)S(1)}, u32[]{:S(2)}, u32[]{:S(2)}) %all-to-all-start.3) | async-done | bytes 131104 | tf_op jit(solution)/shard_map/all_to_all | solution.py:23
  126.8 0.1 reduce_sum.57
  126.9 0.6 multiply_reduce_fusion.1
  128.2 0.6 broadcast_in_dim.31
  128.8 3.9 %all-to-all-start.4 = ((f32[32,1,1]{2,1,0:T(1,128)}), f32[32,1,1]{2,1,0:T(1,128)S(1)}, u32[]{:S(2)}, u32[]{:S(2)}) async-start(f32[32,1,1]{2,1,0:T(1,128)} %broadcast_in_dim.31), calls=%async_computation.4 | async-start | bytes 32768 | tf_op jit(solution)/shard_map/all_to_all | solution.py:23
  132.6 0.6 dynamic-slice_bitcast_fusion
  133.2 0.6 dynamic_slice.7
  133.8 7.5 %all-to-all-done.4 = f32[32,1,1]{2,1,0:T(1,128)S(1)} async-done(((f32[32,1,1]{2,1,0:T(1,128)}), f32[32,1,1]{2,1,0:T(1,128)S(1)}, u32[]{:S(2)}, u32[]{:S(2)}) %all-to-all-start.4) | async-done | bytes 160 | tf_op jit(solution)/shard_map/all_to_all | solution.py:23
  141.3 0.6 reduce_sum.59
  (11 shorter events, 0.2 us)
Async XLA Ops:
  0.6 25.1 %copy-start.3 = (bf16[1,48,384]{2,1,0:T(8,128)(2,1)S(1)}, bf16[1,48,384]{2,1,0:T(8,128)(2,1)}, u32[]{:S(2)}) copy-start(bf16[1,48,384]{2,1,0:T(8,128)(2,1)} %param.2) | copy-start | bytes 110596
  0.6 20.2 %collective-permute-start = (bf16[1024,384]{1,0:T(8,128)(2,1)}, bf16[1024,384]{1,0:T(8,128)(2,1)S(1)}, u32[]{:S(2)}, u32[]{:S(2)}) collective-permute-start(bf16[1024,384]{1,0:T(8,128)(2,1)} %param.3), channel_id=1, source_target_pairs={{0,5},{5,0},{1,4},{4,1},{2,7},{7,2},{3,6},{6,3},{8,13},{13,8},{9,1... | collective-permute-start | bytes 2359304 | tf_op jit(solution)/shard_map/ppermute | solution.py:90
  20.8 26.7 %copy-start.1 = (bf16[1024,384]{1,0:T(8,128)(2,1)}, bf16[1024,384]{1,0:T(8,128)(2,1)S(1)}, u32[]{:S(2)}) copy-start(bf16[1024,384]{1,0:T(8,128)(2,1)S(1)} %collective-permute-done) | copy-start | bytes 2359300
  23.6 28.3 %collective-permute-start.1 = (bf16[2048,384]{1,0:T(8,128)(2,1)}, bf16[2048,384]{1,0:T(8,128)(2,1)S(1)}, u32[]{:S(2)}, u32[]{:S(2)}) collective-permute-start(bf16[2048,384]{1,0:T(8,128)(2,1)} %pad_maximum_fusion.1), channel_id=1, source_target_pairs={{0,2},{2,0},{1,3},{3,1},{4,6},{6,4},{5,7},{7,5},{8,10},{10,8},{9,1... | collective-permute-start | bytes 4718600 | tf_op jit(solution)/shard_map/ppermute | solution.py:92
  47.6 20.0 %all-to-all-start.1 = ((bf16[4,384,384]{2,1,0:T(8,128)(2,1)}), bf16[4,384,384]{2,1,0:T(8,128)(2,1)}, u32[]{:S(2)}, u32[]{:S(2)}) async-start(bf16[4,384,384]{2,1,0:T(8,128)(2,1)} %broadcast_in_dim.26), calls=%async_computation.1 | async-start | bytes 2359296 | tf_op jit(solution)/shard_map/all_to_all | solution.py:23
  51.8 1.1 copy-start.2
  81.3 8.3 %copy-start = (f32[4096,1536]{1,0:T(8,128)}, f32[4096,1536]{1,0:T(8,128)S(1)}, u32[]{:S(2)}) copy-start(f32[4096,1536]{1,0:T(8,128)S(1)} %get-tuple-element.8) | copy-start | bytes 75497472
  90.4 13.3 %all-to-all-start.2 = ((f32[32,1,1536]{2,1,0:T(1,128)}), f32[32,1,1536]{2,1,0:T(1,128)S(1)}, u32[]{:S(2)}, u32[]{:S(2)}) async-start(f32[32,1,1536]{2,1,0:T(1,128)} %broadcast_in_dim.27), calls=%async_computation.2 | async-start | bytes 393216 | tf_op jit(solution)/shard_map/all_to_all | solution.py:23
  114.4 12.4 %all-to-all-start.3 = ((f32[8,1,4096]{2,1,0:T(1,128)}), f32[8,1,4096]{2,1,0:T(1,128)S(1)}, u32[]{:S(2)}, u32[]{:S(2)}) async-start(f32[8,1,4096]{2,1,0:T(1,128)} %broadcast_in_dim.30), calls=%async_computation.3 | async-start | bytes 262144 | tf_op jit(solution)/shard_map/all_to_all | solution.py:23
  128.8 12.5 %all-to-all-start.4 = ((f32[32,1,1]{2,1,0:T(1,128)}), f32[32,1,1]{2,1,0:T(1,128)S(1)}, u32[]{:S(2)}, u32[]{:S(2)}) async-start(f32[32,1,1]{2,1,0:T(1,128)} %broadcast_in_dim.31), calls=%async_computation.4 | async-start | bytes 32768 | tf_op jit(solution)/shard_map/all_to_all | solution.py:23

commit v2 on v0

v2 whole, which is shorter than its diff:
```python
import functools

import jax
import jax.numpy as jnp
from jax import lax
from jax.experimental import pallas as pl
from jax.experimental.pallas import tpu as pltpu
from jax.sharding import Mesh
from jax.sharding import PartitionSpec as P


BLK = ("x", "z", "yh", "core")
RING_Y = ("yh", "rep")
COLUMN = ("yh", "core", "rep")
PLANE = ("x", "z")
LOG2E = 1.4426950408889634
VB = 256
FB = 256
LANES = 128


def exchange(array, axis):
    return lax.all_to_all(array, axis, split_axis=0, concat_axis=0, tiled=True)


def spread(array, axis):
    n = lax.axis_size(axis)
    return exchange(jnp.broadcast_to(array, (n, *array.shape)), axis)


def shifted(array, step):
    n = lax.axis_size("x")
    return lax.ppermute(array, "x", [(i, (i + step) % n) for i in range(n)])


def in_vmem(count):
    return [pl.BlockSpec(memory_space=pltpu.VMEM)] * count


def scores_into(scratch, codes, start, frames):
    s = lax.dot_general(
        codes[pl.ds(start, VB), :],
        frames,
        (((1,), (1,)), ((), ())),
        preferred_element_type=jnp.float32,
    )
    scratch[...] = s
    return jnp.max(s, axis=0, keepdims=True)


def tile(frames_of, chunks, width, codes, probs, high, total, scratch):
    steps = [(c, b) for c in codes for b in range(0, c.shape[0], VB)]

    def chunk(i, top):
        lanes = pl.ds(pl.multiple_of(i * width, LANES), width)
        after = jnp.minimum(i + 1, chunks - 1)
        for k in range(len(steps)):
            if k + 1 < len(steps):
                ref, start = steps[k + 1]
                later = scores_into(scratch[(k + 1) % 2], ref, start, frames_of(i))
            else:
                ref, start = steps[0]
                later = scores_into(scratch[0], ref, start, frames_of(after))
            p = jnp.exp2((scratch[k % 2][...] - top) * LOG2E)
            probs[pl.ds(k * VB, VB), lanes] = p
            high[pl.ds(k, 1), lanes] = top
            total[pl.ds(k, 1), lanes] = jnp.sum(p, axis=0, keepdims=True)
            top = later
        return top

    first = scores_into(scratch[0], steps[0][0], steps[0][1], frames_of(0))
    lax.fori_loop(0, chunks, chunk, first)


def merged(high, total):
    top = jnp.max(high, axis=0, keepdims=True)
    return top + jnp.log(
        jnp.sum(total * jnp.exp(high - top), axis=0, keepdims=True)
    )


def own_kernel(line, c0, c1, c2, c3, probs, high, total, sa, sb):
    def frames_of(i):
        return line[pl.ds(0, FB), :]

    tile(frames_of, 1, FB, (c0, c1, c2, c3), probs, high, total, (sa, sb))


def near_kernel(before, after, c0, c1, c2, c3, probs, high, total, joined, sa, sb):
    count = before.shape[0]
    joined[pl.ds(0, count), :] = before[...]
    joined[pl.ds(count, count), :] = after[...]

    def frames_of(i):
        return joined[pl.ds(pl.multiple_of(i * FB, FB), FB), :]

    chunks = 2 * count // FB
    tile(frames_of, chunks, FB, (c0, c1, c2, c3), probs, high, total, (sa, sb))


def place(line, count):
    at = lax.rem(lax.axis_index("x") + line, lax.axis_size("x")) * count
    return pl.multiple_of(at, LANES)


def far_kernel(
    far, line, c0, c1, c2, c3, own_high, own_total, near_high, near_total,
    probs, high, lse_out, total, joined, sa, sb,
):
    count = far.shape[0]
    left = count - FB
    joined[pl.ds(0, count), :] = far[...]
    joined[pl.ds(count, left), :] = line[pl.ds(FB, left), :]

    def frames_of(i):
        return joined[pl.ds(pl.multiple_of(i * FB, FB), FB), :]

    chunks = (count + left) // FB
    tile(frames_of, chunks, FB, (c0, c1, c2, c3), probs, high, total, (sa, sb))

    def put(start, lse):
        lanes = pl.ds(start, lse.shape[1])
        for k in range(lse_out.shape[0]):
            lse_out[k, :, lanes] = lse

    put(place(0, count), merged(own_high[...], own_total[...]))
    near = merged(near_high[...], near_total[...])
    put(place(3, count), near[:, :count])
    put(place(1, count), near[:, count:])
    last = merged(high[...], total[...])
    put(place(2, count), last[:, :count])
    put(pl.multiple_of(place(0, count) + FB, LANES), last[:, count:])


def cost_of(count, protos, width):
    return pl.CostEstimate(
        flops=2 * count * protos * width,
        bytes_accessed=4 * count * protos,
        transcendentals=count * protos,
    )


def tile_call(kernel, tensors, codes, stats, count, last=None):
    width = codes[0].shape[1]
    protos = sum(c.shape[0] for c in codes)
    blocks = protos // VB
    f32, bf16 = jnp.float32, jnp.bfloat16
    stat = jax.ShapeDtypeStruct((blocks, count), f32)
    scratch = [pltpu.VMEM((VB, FB), f32)] * 2
    if len(tensors) > 1:
        scratch = [pltpu.VMEM((count, width), bf16)] + scratch
    if last is not None:
        scratch = [pltpu.VMEM((blocks, count), f32)] + scratch
    return pl.pallas_call(
        kernel,
        in_specs=in_vmem(len(tensors) + len(codes) + len(stats)),
        out_specs=in_vmem(3),
        out_shape=[
            jax.ShapeDtypeStruct((protos, count), f32),
            stat,
            stat if last is None else jax.ShapeDtypeStruct(last, f32),
        ],
        scratch_shapes=scratch,
        compiler_params=pltpu.CompilerParams(vmem_limit_bytes=8 * 1024 * 1024),
        cost_estimate=cost_of(count, protos, width),
    )(*tensors, *codes, *stats)


def usage_kernel(
    own_probs, own_high, near_probs, near_high, far_probs, far_high, parts,
    lse_out, usage_out,
):
    count = near_probs.shape[1] // 2
    left = count - FB
    groups = near_probs.shape[0] // LANES
    each = groups // 4
    peak = parts[0]
    for k in range(1, parts.shape[0]):
        peak = jnp.maximum(peak, parts[k])
    mass = jnp.exp(parts[0] - peak)
    for k in range(1, parts.shape[0]):
        mass = mass + jnp.exp(parts[k] - peak)
    lse_out[...] = peak + jnp.log(mass)

    yh, core = lax.axis_index("yh"), lax.axis_index("core")
    held = []

    def hold(probs, high, at, size, start):
        lse = lse_out[:, pl.ds(start, size)]
        held.append((probs, at, size, jnp.exp(high[:, at : at + size] - lse)))

    hold(own_probs, own_high, 0, FB, place(0, count))
    hold(near_probs, near_high, 0, count, place(3, count))
    hold(near_probs, near_high, count, count, place(1, count))
    hold(far_probs, far_high, 0, count, place(2, count))
    rest = pl.multiple_of(place(0, count) + FB, LANES)
    hold(far_probs, far_high, count, left, rest)

    for g in range(groups):
        block = g * LANES // VB
        acc = None
        for ref, at, size, weight in held:
            for j in range(0, size, LANES):
                term = (
                    ref[pl.ds(g * LANES, LANES), pl.ds(at + j, LANES)]
                    * weight[block : block + 1, j : j + LANES]
                )
                acc = term if acc is None else acc + term
        line = jnp.sum(acc.T, axis=0, keepdims=True)
        flip = g // each
        far, beside = flip // 2, flip % 2
        owner = jnp.where(yh == 1, 2 - 2 * far, 2 * far) + jnp.where(
            core == 1, 1 - beside, beside
        )
        for k in range(usage_out.shape[0]):
            usage_out[k, pl.ds(owner * each + g % each, 1), :] = line


def usage_of(held, parts, copies):
    protos = held[0].shape[0]
    total = parts.shape[2]
    f32 = jnp.float32
    return pl.pallas_call(
        usage_kernel,
        in_specs=in_vmem(len(held) + 1),
        out_specs=in_vmem(2),
        out_shape=[
            jax.ShapeDtypeStruct((1, total), f32),
            jax.ShapeDtypeStruct((copies, protos // LANES, LANES), f32),
        ],
        compiler_params=pltpu.CompilerParams(vmem_limit_bytes=8 * 1024 * 1024),
        cost_estimate=pl.CostEstimate(
            flops=2 * protos * total,
            bytes_accessed=4 * protos * total,
            transcendentals=total * protos // VB,
        ),
        name="usage_of",
    )(*held, parts)


def entropy_kernel(embeddings, counts, column_out, term_out):
    column = counts[0]
    for k in range(1, counts.shape[0]):
        column = column + counts[k]
    column_out[...] = column
    mean_use = column / embeddings
    term = -jnp.sum(mean_use * jnp.log(mean_use + 1e-07), keepdims=True)
    term_out[...] = jnp.broadcast_to(term[None], term_out.shape)


def entropy_of(counts, embeddings, copies):
    f32 = jnp.float32
    return pl.pallas_call(
        functools.partial(entropy_kernel, embeddings),
        in_specs=in_vmem(1),
        out_specs=in_vmem(2),
        out_shape=[
            jax.ShapeDtypeStruct(counts.shape[1:], f32),
            jax.ShapeDtypeStruct((copies, 1, LANES), f32),
        ],
        compiler_params=pltpu.CompilerParams(vmem_limit_bytes=4 * 1024 * 1024),
        name="entropy_of",
    )(counts)


def per_device(frames, codebook):
    own = frames[0]
    shard_rows, width = own.shape
    owned = codebook.shape[0]
    yh, core = lax.axis_index("yh"), lax.axis_index("core")
    plane, ring = lax.axis_size(PLANE), lax.axis_size(COLUMN)
    swap = [(0, 1), (1, 0)]

    opposite = lax.ppermute(codebook, RING_Y, [(0, 3), (3, 0), (1, 2), (2, 1)])
    beside = lax.ppermute(codebook, "core", swap)
    line = spread(own, "z").reshape(-1, width)
    far = shifted(line, 2)
    before = shifted(line, 1)
    after = shifted(line, -1)
    opposite, line = lax.optimization_barrier((opposite, line))
    across = lax.ppermute(opposite, "core", swap)

    count = line.shape[0]
    codes = (codebook, beside, opposite, across)
    own_probs, own_high, own_total = tile_call(
        own_kernel, (line,), codes, (), FB
    )
    near_probs, near_high, near_total = tile_call(
        near_kernel, (before, after), codes, (), 2 * count
    )
    stats = (own_high, own_total, near_high, near_total)
    far_probs, far_high, part = tile_call(
        far_kernel, (far, line), codes, stats, 2 * count - FB,
        (plane, 1, 4 * count),
    )
    parts = exchange(part, PLANE)
    held = (own_probs, own_high, near_probs, near_high, far_probs, far_high)
    lse, usage = usage_of(held, parts, ring)
    embeddings = shard_rows * lax.axis_size(BLK) * lax.axis_size("rep")
    column, term = entropy_of(exchange(usage, COLUMN), embeddings, plane)

    at = lax.axis_index(PLANE) * shard_rows
    lse_own = lax.dynamic_slice(lse, (0, at), (1, shard_rows))
    usage_own = lax.dynamic_slice_in_dim(
        column, (2 * yh + core) * (owned // LANES), owned // LANES, 0
    ).reshape(owned)
    entropy = jnp.sum(exchange(term, PLANE)[:, 0, 0])
    return (lse_own, usage_own, entropy)


def solution(mesh):
    split = Mesh(
        mesh.devices.reshape(4, 8, 2, 2, mesh.shape["rep"]),
        ("x", "z", "yh", "core", "rep"),
    )
    return jax.shard_map(
        per_device,
        mesh=split,
        in_specs=(P("rep", BLK, None), P(BLK, None)),
        out_specs=(P("rep", BLK), P(BLK), P()),
        check_vma=False,
    )
```

time: 266 us -> 95.8 us (0.36)
  waiting for transfers between devices: 132 us -> 27.9 us
  blocking collectives: 84.3 us -> 14.1 us
  starting transfers between devices: 3.26 us -> 35.5 us
  other arithmetic: 16 us -> 0.63 us
  between operations: 14.8 us -> 0.66 us
  matrix products: 14 us -> 0 us
  Pallas kernels: 0 us -> 12.6 us
    all_gather x1 -> x0, waiting for transfers between devices: 129 us -> none  [per_device(): lax.all_gather(frame_rows, BLK, axis=0, tiled=True)]
    all_gather x4 -> x0, blocking collectives: 45.7 us -> none  [gathered_once(): both, at, found = (lax.all_gather(jnp.concatenate(lines), axis), 0, {})]
    psum x4 -> x0, blocking collectives: 38.5 us -> none  [one_axis_at_a_time(): return functools.reduce(lax.psum, axes, array)]
    all_to_all x1 -> x3, starting transfers between devices: 3.22 us -> 23.7 us  [exchange(): return lax.all_to_all(array, axis, split_axis=0, concat_axis=0, tiled=True)]
    all_to_all x1 -> x3, waiting for transfers between devices: 2.64 us -> 22.1 us  [exchange(): return lax.all_to_all(array, axis, split_axis=0, concat_axis=0, tiled=True)]
    reduce_sum x4 -> x1, other arithmetic: 14.8 us -> 0.63 us  [per_device(): entropy = jnp.sum(exchange(term, PLANE)[:, 0, 0])]
    all_to_all x0 -> x1, blocking collectives: none -> 14.1 us  [exchange(): return lax.all_to_all(array, axis, split_axis=0, concat_axis=0, tiled=True)]
    dot_general x1 -> x0, matrix products: 14 us -> none  [score_block(): lax.dot_general(moving, codebook, (((1,), (1,)), ((), ())), preferred_ele...]
  transfers between devices with their start and end apart: 2 -> 9, of which waited for: 2 -> 5; matrix products, arithmetic and copies ran while one was open for 0% -> 3% of each run, Pallas kernels for 0% -> 6%
where the time goes in v2:
time: 95.8 us; the launch traced here: 95.2 us
  starting transfers between devices  35.5 us (37%)
  waiting for transfers between devices  27.9 us (29%)
  blocking collectives  14.1 us (15%)
  Pallas kernels  12.6 us (13%)
  local copies, waits for them, and re-layouts  3.81 us (4%)
    all_to_all x3, starting transfers between devices, exchange(): return lax.all_to_all(array, axis, split_axis=0, concat_axis=0, tiled=True)  23.7 us
    all_to_all x3, waiting for transfers between devices, exchange(): return lax.all_to_all(array, axis, split_axis=0, concat_axis=0, tiled=True)  22.1 us
    all_to_all x1, blocking collectives, exchange(): return lax.all_to_all(array, axis, split_axis=0, concat_axis=0, tiled=True)  14.1 us
    pallas_call x3, Pallas kernels, tile_call(): pl.pallas_call(kernel, in_specs=in_vmem(len(tensors) + len(codes) + len(s...  9.08 us
    ppermute x3, waiting for transfers between devices, shifted(): return lax.ppermute(array, 'x', [(i, (i + step) % n) for i in range(n)])  5.82 us
    ppermute x3, starting transfers between devices, shifted(): return lax.ppermute(array, 'x', [(i, (i + step) % n) for i in range(n)])  4.21 us
    ppermute x1, starting transfers between devices, per_device(): opposite = lax.ppermute(codebook, RING_Y, [(0, 3), (3, 0), (1, 2), (2, 1)])  3.64 us
    pallas_call x1, Pallas kernels, usage_of(): pl.pallas_call(usage_kernel, in_specs=in_vmem(len(held) + 1), out_specs=i...  2.77 us
  transfers between devices with their start and end apart: 9, of which 5 were waited for; matrix products, arithmetic and copies ran while one was open for 3% of the time, Pallas kernels for 6%

profile of v2, /device:TPU:1, one launch (start us, length us, event | category | flops | bytes accessed | tf_op | source)
XLA Modules:
  0.0 95.2 jit_solution(17056024432220442371)
XLA Ops:
  0.6 3.6 %collective-permute-start = (bf16[1024,384]{1,0:T(8,128)(2,1)}, bf16[1024,384]{1,0:T(8,128)(2,1)S(1)}, u32[]{:S(2)}, u32[]{:S(2)}) collective-permute-start(bf16[1024,384]{1,0:T(8,128)(2,1)} %c0.5), channel_id=1, source_target_pairs={{0,5},{5,0},{1,4},{4,1},{2,7},{7,2},{3,6},{6,3},{8,13},{13,8},{9,1... | collective-permute-start | bytes 2359304 | tf_op jit(solution)/shard_map/ppermute | solution.py:274
  4.3 1.5 %broadcast_in_dim.3 = bf16[8,48,384]{2,1,0:T(8,128)(2,1)} broadcast(bf16[48,384]{1,0:T(8,128)(2,1)} %bitcast.9), dimensions={1,2} | broadcast | bytes 331776 | tf_op jit(solution)/shard_map/broadcast_in_dim | solution.py:28
  5.8 8.2 %all-to-all-start = ((bf16[8,48,384]{2,1,0:T(8,128)(2,1)}), bf16[8,48,384]{2,1,0:T(8,128)(2,1)S(1)}, u32[]{:S(2)}, u32[]{:S(2)}) async-start(bf16[8,48,384]{2,1,0:T(8,128)(2,1)} %broadcast_in_dim.3), calls=%async_computation | async-start | bytes 589824 | tf_op jit(solution)/shard_map/all_to_all | solution.py:23
  13.9 1.2 %collective-permute-start.1 = (bf16[1024,384]{1,0:T(8,128)(2,1)}, bf16[1024,384]{1,0:T(8,128)(2,1)S(1)}, u32[]{:S(2)}, u32[]{:S(2)}) collective-permute-start(bf16[1024,384]{1,0:T(8,128)(2,1)} %c0.5), channel_id=1, source_target_pairs={{0,2},{2,0},{1,3},{3,1},{4,6},{6,4},{5,7},{7,5},{8,10},{10,8},{9,1... | collective-permute-start | bytes 2359304 | tf_op jit(solution)/shard_map/ppermute | solution.py:275
  15.2 9.6 %all-to-all-done = bf16[8,48,384]{2,1,0:T(8,128)(2,1)S(1)} async-done(((bf16[8,48,384]{2,1,0:T(8,128)(2,1)}), bf16[8,48,384]{2,1,0:T(8,128)(2,1)S(1)}, u32[]{:S(2)}, u32[]{:S(2)}) %all-to-all-start) | async-done | bytes 294944 | tf_op jit(solution)/shard_map/all_to_all | solution.py:23
  24.7 0.0 collective-permute-done.c2
  24.7 2.7 %collective-permute-start.2 = (bf16[1024,384]{1,0:T(8,128)(2,1)S(1)}, bf16[1024,384]{1,0:T(8,128)(2,1)S(1)}, u32[]{:S(2)}, u32[]{:S(2)}) collective-permute-start(bf16[1024,384]{1,0:T(8,128)(2,1)S(1)} %collective-permute-done.c2), channel_id=1, source_target_pairs={{0,2},{2,0},{1,3},{3,1},{4,6},{6,4},{5,7},{7,5},{8,10},{10,8},{9,1... | collective-permute-start | bytes 2359304 | tf_op jit(solution)/shard_map/ppermute | solution.py:281
  27.5 1.2 %collective-permute-start.3 = (bf16[384,384]{1,0:T(8,128)(2,1)S(1)}, bf16[384,384]{1,0:T(8,128)(2,1)S(1)}, u32[]{:S(2)}, u32[]{:S(2)}) collective-permute-start(bf16[384,384]{1,0:T(8,128)(2,1)S(1)} %bitcast.4), channel_id=1, source_target_pairs={{0,64},{64,128},{128,192},{192,0},{1,65},{65,129},{129,193},{193,1... | collective-permute-start | bytes 884744 | tf_op jit(solution)/shard_map/ppermute | solution.py:33
  28.7 1.5 %collective-permute-start.4 = (bf16[384,384]{1,0:T(8,128)(2,1)S(1)}, bf16[384,384]{1,0:T(8,128)(2,1)S(1)}, u32[]{:S(2)}, u32[]{:S(2)}) collective-permute-start(bf16[384,384]{1,0:T(8,128)(2,1)S(1)} %bitcast.5), channel_id=1, source_target_pairs={{0,192},{64,0},{128,64},{192,128},{1,193},{65,1},{129,65},{193,129... | collective-permute-start | bytes 884744 | tf_op jit(solution)/shard_map/ppermute | solution.py:33
  30.2 1.5 %collective-permute-start.5 = (bf16[384,384]{1,0:T(8,128)(2,1)S(1)}, bf16[384,384]{1,0:T(8,128)(2,1)S(1)}, u32[]{:S(2)}, u32[]{:S(2)}) collective-permute-start(bf16[384,384]{1,0:T(8,128)(2,1)S(1)} %bitcast.6), channel_id=1, source_target_pairs={{0,128},{64,192},{128,0},{192,64},{1,129},{65,193},{129,1},{193,65... | collective-permute-start | bytes 884744 | tf_op jit(solution)/shard_map/ppermute | solution.py:33
  31.7 0.0 collective-permute-done.1.c1
  31.7 0.0 collective-permute-done.2.c3
  31.7 0.0 copy-start
  31.7 1.1 %copy-done = bf16[1024,384]{1,0:T(8,128)(2,1)S(1)} copy-done((bf16[1024,384]{1,0:T(8,128)(2,1)S(1)}, bf16[1024,384]{1,0:T(8,128)(2,1)}, u32[]{:S(2)}) %copy-start) | copy-done | bytes 786456
  32.8 1.4 %shard_map.49 = (f32[4096,256]{1,0:T(8,128)S(1)}, f32[16,256]{1,0:T(8,128)S(1)}, f32[16,256]{1,0:T(8,128)S(1)}) custom-call(bf16[384,384]{1,0:T(8,128)(2,1)S(1)} %bitcast.7, bf16[1024,384]{1,0:T(8,128)(2,1)S(1)} %copy-done, bf16[1024,384]{1,0:T(8,128)(2,1)S(1)} %collective-permute-done.1.c1, bf16[1024,384]{1,0:T(8,128)(2,1)S(1)} %collective-permute-done.c2, ...), custom_call_target="tpu_custom_call" | custom-call | flops 805306368 | bytes 4194304 | tf_op jit(solution)/shard_map/pallas_call | solution.py:154
  34.3 3.0 %collective-permute-done.3.before = bf16[384,384]{1,0:T(8,128)(2,1)S(1)} collective-permute-done((bf16[384,384]{1,0:T(8,128)(2,1)S(1)}, bf16[384,384]{1,0:T(8,128)(2,1)S(1)}, u32[]{:S(2)}, u32[]{:S(2)}) %collective-permute-start.3) | collective-permute-done | bytes 294944 | tf_op jit(solution)/shard_map/ppermute | solution.py:33
  37.3 0.0 collective-permute-done.4.after
  37.3 4.5 %shard_map.50 = (f32[4096,768]{1,0:T(8,128)S(1)}, f32[16,768]{1,0:T(8,128)S(1)}, f32[16,768]{1,0:T(8,128)S(1)}) custom-call(bf16[384,384]{1,0:T(8,128)(2,1)S(1)} %collective-permute-done.3.before, bf16[384,384]{1,0:T(8,128)(2,1)S(1)} %collective-permute-done.4.after, bf16[1024,384]{1,0:T(8,128)(2,1)S(1)} %copy-done, ...), custom_call_target="tpu_custom_call" | custom-call | flops 2415919104 | bytes 12582912 | tf_op jit(solution)/shard_map/pallas_call | solution.py:154
  41.7 2.8 %collective-permute-done.5.far = bf16[384,384]{1,0:T(8,128)(2,1)S(1)} collective-permute-done((bf16[384,384]{1,0:T(8,128)(2,1)S(1)}, bf16[384,384]{1,0:T(8,128)(2,1)S(1)}, u32[]{:S(2)}, u32[]{:S(2)}) %collective-permute-start.5) | collective-permute-done | bytes 294944 | tf_op jit(solution)/shard_map/ppermute | solution.py:33
  44.6 3.2 %shard_map.51 = (f32[4096,512]{1,0:T(8,128)S(1)}, f32[16,512]{1,0:T(8,128)S(1)}, f32[32,1,1536]{2,1,0:T(1,128)S(1)}) custom-call(bf16[384,384]{1,0:T(8,128)(2,1)S(1)} %collective-permute-done.5.far, bf16[384,384]{1,0:T(8,128)(2,1)S(1)} %bitcast.8, bf16[1024,384]{1,0:T(8,128)(2,1)S(1)} %copy-done, bf16[1024,384]{1,0:T(8,128)(2,1)S(1)} %collective-permute-done.1.c1, ...), custom_call_target="tpu_custom_call" | custom-call | flops 1610612736 | bytes 8388608 | tf_op jit(solution)/shard_map/pallas_call | solution.py:154
  47.7 14.1 %all_to_all.20.parts = f32[32,1,1536]{2,1,0:T(1,128)S(1)} all-to-all(f32[32,1,1536]{2,1,0:T(1,128)S(1)} %get-tuple-element.28), channel_id=1, replica_groups=mesh['x'=4,'z'=8,'yh'=2,'core'=2,'rep'=2] {'x','z'}, dimensions={0} | all-to-all | bytes 393216 | tf_op jit(solution)/shard_map/all_to_all | solution.py:23
  61.9 2.8 %usage_of.1 = (f32[1,1536]{1,0:T(1,128)S(1)}, f32[8,32,128]{2,1,0:T(8,128)}) custom-call(f32[4096,256]{1,0:T(8,128)S(1)} %get-tuple-element.20.own_probs, f32[16,256]{1,0:T(8,128)S(1)} %get-tuple-element.21.own_high, f32[4096,768]{1,0:T(8,128)S(1)} %get-tuple-element.22.near_probs, f32[16,768]{1,0:T(8,128)S(1)} %get-tuple-element.23.near_high, ...), custom_call_target="tpu_custom_call" | custom-call | flops 12582912 | bytes 25165824 | tf_op jit(solution)/shard_map/usage_of/pallas_call | solution.py:223
  64.7 11.5 %all-to-all-start.2 = ((f32[8,32,128]{2,1,0:T(8,128)}), f32[8,32,128]{2,1,0:T(8,128)S(1)}, u32[]{:S(2)}, u32[]{:S(2)}) async-start(f32[8,32,128]{2,1,0:T(8,128)} %get-tuple-element.30), calls=%async_computation.2 | async-start | bytes 262144 | tf_op jit(solution)/shard_map/all_to_all | solution.py:23
  76.1 0.6 constant_dynamic-slice_fusion
  76.7 4.5 %all-to-all-done.2.counts = f32[8,32,128]{2,1,0:T(8,128)S(1)} async-done(((f32[8,32,128]{2,1,0:T(8,128)}), f32[8,32,128]{2,1,0:T(8,128)S(1)}, u32[]{:S(2)}, u32[]{:S(2)}) %all-to-all-start.2) | async-done | bytes 131104 | tf_op jit(solution)/shard_map/all_to_all | solution.py:23
  81.2 0.7 entropy_of.1
  82.0 4.0 %all-to-all-start.3 = ((f32[32,1,128]{2,1,0:T(1,128)}), f32[32,1,128]{2,1,0:T(1,128)S(1)}, u32[]{:S(2)}, u32[]{:S(2)}) async-start(f32[32,1,128]{2,1,0:T(1,128)} %get-tuple-element.32), calls=%async_computation.3 | async-start | bytes 32768 | tf_op jit(solution)/shard_map/all_to_all | solution.py:23
  85.9 0.6 dynamic-slice_bitcast_fusion
  86.5 8.1 %all-to-all-done.3 = f32[32,1,128]{2,1,0:T(1,128)S(1)} async-done(((f32[32,1,128]{2,1,0:T(1,128)}), f32[32,1,128]{2,1,0:T(1,128)S(1)}, u32[]{:S(2)}, u32[]{:S(2)}) %all-to-all-start.3) | async-done | bytes 16416 | tf_op jit(solution)/shard_map/all_to_all | solution.py:23
  94.6 0.6 slice_reduce_fusion
Async XLA Ops:
  0.6 24.1 %collective-permute-start = (bf16[1024,384]{1,0:T(8,128)(2,1)}, bf16[1024,384]{1,0:T(8,128)(2,1)S(1)}, u32[]{:S(2)}, u32[]{:S(2)}) collective-permute-start(bf16[1024,384]{1,0:T(8,128)(2,1)} %c0.5), channel_id=1, source_target_pairs={{0,5},{5,0},{1,4},{4,1},{2,7},{7,2},{3,6},{6,3},{8,13},{13,8},{9,1... | collective-permute-start | bytes 2359304 | tf_op jit(solution)/shard_map/ppermute | solution.py:274
  5.8 19.0 %all-to-all-start = ((bf16[8,48,384]{2,1,0:T(8,128)(2,1)}), bf16[8,48,384]{2,1,0:T(8,128)(2,1)S(1)}, u32[]{:S(2)}, u32[]{:S(2)}) async-start(bf16[8,48,384]{2,1,0:T(8,128)(2,1)} %broadcast_in_dim.3), calls=%async_computation | async-start | bytes 589824 | tf_op jit(solution)/shard_map/all_to_all | solution.py:23
  13.9 17.8 %collective-permute-start.1 = (bf16[1024,384]{1,0:T(8,128)(2,1)}, bf16[1024,384]{1,0:T(8,128)(2,1)S(1)}, u32[]{:S(2)}, u32[]{:S(2)}) collective-permute-start(bf16[1024,384]{1,0:T(8,128)(2,1)} %c0.5), channel_id=1, source_target_pairs={{0,2},{2,0},{1,3},{3,1},{4,6},{6,4},{5,7},{7,5},{8,10},{10,8},{9,1... | collective-permute-start | bytes 2359304 | tf_op jit(solution)/shard_map/ppermute | solution.py:275
  24.7 7.0 %collective-permute-start.2 = (bf16[1024,384]{1,0:T(8,128)(2,1)S(1)}, bf16[1024,384]{1,0:T(8,128)(2,1)S(1)}, u32[]{:S(2)}, u32[]{:S(2)}) collective-permute-start(bf16[1024,384]{1,0:T(8,128)(2,1)S(1)} %collective-permute-done.c2), channel_id=1, source_target_pairs={{0,2},{2,0},{1,3},{3,1},{4,6},{6,4},{5,7},{7,5},{8,10},{10,8},{9,1... | collective-permute-start | bytes 2359304 | tf_op jit(solution)/shard_map/ppermute | solution.py:281
  27.5 9.8 %collective-permute-start.3 = (bf16[384,384]{1,0:T(8,128)(2,1)S(1)}, bf16[384,384]{1,0:T(8,128)(2,1)S(1)}, u32[]{:S(2)}, u32[]{:S(2)}) collective-permute-start(bf16[384,384]{1,0:T(8,128)(2,1)S(1)} %bitcast.4), channel_id=1, source_target_pairs={{0,64},{64,128},{128,192},{192,0},{1,65},{65,129},{129,193},{193,1... | collective-permute-start | bytes 884744 | tf_op jit(solution)/shard_map/ppermute | solution.py:33
  28.7 8.6 %collective-permute-start.4 = (bf16[384,384]{1,0:T(8,128)(2,1)S(1)}, bf16[384,384]{1,0:T(8,128)(2,1)S(1)}, u32[]{:S(2)}, u32[]{:S(2)}) collective-permute-start(bf16[384,384]{1,0:T(8,128)(2,1)S(1)} %bitcast.5), channel_id=1, source_target_pairs={{0,192},{64,0},{128,64},{192,128},{1,193},{65,1},{129,65},{193,129... | collective-permute-start | bytes 884744 | tf_op jit(solution)/shard_map/ppermute | solution.py:33
  30.2 14.4 %collective-permute-start.5 = (bf16[384,384]{1,0:T(8,128)(2,1)S(1)}, bf16[384,384]{1,0:T(8,128)(2,1)S(1)}, u32[]{:S(2)}, u32[]{:S(2)}) collective-permute-start(bf16[384,384]{1,0:T(8,128)(2,1)S(1)} %bitcast.6), channel_id=1, source_target_pairs={{0,128},{64,192},{128,0},{192,64},{1,129},{65,193},{129,1},{193,65... | collective-permute-start | bytes 884744 | tf_op jit(solution)/shard_map/ppermute | solution.py:33
  31.7 1.1 %copy-start = (bf16[1024,384]{1,0:T(8,128)(2,1)S(1)}, bf16[1024,384]{1,0:T(8,128)(2,1)}, u32[]{:S(2)}) copy-start(bf16[1024,384]{1,0:T(8,128)(2,1)} %c0.5) | copy-start | bytes 2359300
  64.7 16.6 %all-to-all-start.2 = ((f32[8,32,128]{2,1,0:T(8,128)}), f32[8,32,128]{2,1,0:T(8,128)S(1)}, u32[]{:S(2)}, u32[]{:S(2)}) async-start(f32[8,32,128]{2,1,0:T(8,128)} %get-tuple-element.30), calls=%async_computation.2 | async-start | bytes 262144 | tf_op jit(solution)/shard_map/all_to_all | solution.py:23
  82.0 12.6 %all-to-all-start.3 = ((f32[32,1,128]{2,1,0:T(1,128)}), f32[32,1,128]{2,1,0:T(1,128)S(1)}, u32[]{:S(2)}, u32[]{:S(2)}) async-start(f32[32,1,128]{2,1,0:T(1,128)} %get-tuple-element.32), calls=%async_computation.3 | async-start | bytes 32768 | tf_op jit(solution)/shard_map/all_to_all | solution.py:23

commit v3 on v2

--- a/solution.py
+++ b/solution.py
@@ -14,8 +14,7 @@
 COLUMN = ("yh", "core", "rep")
 PLANE = ("x", "z")
 LOG2E = 1.4426950408889634
-VB = 256
-FB = 256
+HELD = 256
 LANES = 128
 
 
@@ -37,39 +36,43 @@
     return [pl.BlockSpec(memory_space=pltpu.VMEM)] * count
 
 
-def scores_into(scratch, codes, start, frames):
-    s = lax.dot_general(
-        codes[pl.ds(start, VB), :],
-        frames,
-        (((1,), (1,)), ((), ())),
+def scores_into(scratch, codes, start, turned):
+    s = jnp.dot(
+        codes[pl.ds(start, scratch.shape[0]), :],
+        turned[...],
         preferred_element_type=jnp.float32,
     )
     scratch[...] = s
     return jnp.max(s, axis=0, keepdims=True)
 
 
-def tile(frames_of, chunks, width, codes, probs, high, total, scratch):
-    steps = [(c, b) for c in codes for b in range(0, c.shape[0], VB)]
-
-    def chunk(i, top):
-        lanes = pl.ds(pl.multiple_of(i * width, LANES), width)
-        after = jnp.minimum(i + 1, chunks - 1)
-        for k in range(len(steps)):
-            if k + 1 < len(steps):
-                ref, start = steps[k + 1]
-                later = scores_into(scratch[(k + 1) % 2], ref, start, frames_of(i))
-            else:
-                ref, start = steps[0]
-                later = scores_into(scratch[0], ref, start, frames_of(after))
-            p = jnp.exp2((scratch[k % 2][...] - top) * LOG2E)
-            probs[pl.ds(k * VB, VB), lanes] = p
-            high[pl.ds(k, 1), lanes] = top
-            total[pl.ds(k, 1), lanes] = jnp.sum(p, axis=0, keepdims=True)
-            top = later
-        return top
-
-    first = scores_into(scratch[0], steps[0][0], steps[0][1], frames_of(0))
-    lax.fori_loop(0, chunks, chunk, first)
+def tile(codes, turned, probs, high, total, scratch, home, arrival):
+    fetch = pltpu.make_async_copy(codes[0], home, arrival)
+    fetch.start()
+    size = scratch[0].shape[0]
+    steps = [
+        (slot, start)
+        for slot in (1, 2, 3, 0)
+        for start in range(0, codes[slot].shape[0], size)
+    ]
+
+    def scores_at(k):
+        slot, start = steps[k]
+        if slot == 0 and start == 0:
+            fetch.wait()
+        ref = home if slot == 0 else codes[slot]
+        return scores_into(scratch[k % 2], ref, start, turned)
+
+    top = scores_at(0)
+    for k in range(len(steps)):
+        later = scores_at(k + 1) if k + 1 < len(steps) else None
+        slot, start = steps[k]
+        at = slot * home.shape[0] + start
+        p = jnp.exp2((scratch[k % 2][...] - top) * LOG2E)
+        probs[pl.ds(at, size), :] = p
+        high[pl.ds(at // size, 1), :] = top
+        total[pl.ds(at // size, 1), :] = jnp.sum(p, axis=0, keepdims=True)
+        top = later
 
 
 def merged(high, total):
@@ -79,23 +82,30 @@
     )
 
 
-def own_kernel(line, c0, c1, c2, c3, probs, high, total, sa, sb):
-    def frames_of(i):
-        return line[pl.ds(0, FB), :]
-
-    tile(frames_of, 1, FB, (c0, c1, c2, c3), probs, high, total, (sa, sb))
-
-
-def near_kernel(before, after, c0, c1, c2, c3, probs, high, total, joined, sa, sb):
-    count = before.shape[0]
-    joined[pl.ds(0, count), :] = before[...]
-    joined[pl.ds(count, count), :] = after[...]
-
-    def frames_of(i):
-        return joined[pl.ds(pl.multiple_of(i * FB, FB), FB), :]
-
-    chunks = 2 * count // FB
-    tile(frames_of, chunks, FB, (c0, c1, c2, c3), probs, high, total, (sa, sb))
+def own_kernel(
+    line, c0, c1, c2, c3, probs, high, total, turned, sa, sb, home, arrival
+):
+    turned[...] = line[pl.ds(0, HELD), :].T
+    codes = (c0, c1, c2, c3)
+    tile(codes, turned, probs, high, total, (sa, sb), home, arrival)
+
+
+def join(pieces, joined, turned):
+    at = 0
+    for ref, start in pieces:
+        size = ref.shape[0] - start
+        joined[pl.ds(at, size), :] = ref[pl.ds(start, size), :]
+        at += size
+    turned[...] = joined[...].T
+
+
+def near_kernel(
+    b0, b1, a0, a1, c0, c1, c2, c3, probs, high, total,
+    turned, sa, sb, home, arrival, joined,
+):
+    join([(b0, 0), (b1, 0), (a0, 0), (a1, 0)], joined, turned)
+    codes = (c0, c1, c2, c3)
+    tile(codes, turned, probs, high, total, (sa, sb), home, arrival)
 
 
 def place(line, count):
@@ -104,19 +114,13 @@
 
 
 def far_kernel(
-    far, line, c0, c1, c2, c3, own_high, own_total, near_high, near_total,
-    probs, high, lse_out, total, joined, sa, sb,
+    f0, f1, line, c0, c1, c2, c3, own_high, own_total, near_high, near_total,
+    probs, high, lse_out, total, turned, sa, sb, home, arrival, joined,
 ):
-    count = far.shape[0]
-    left = count - FB
-    joined[pl.ds(0, count), :] = far[...]
-    joined[pl.ds(count, left), :] = line[pl.ds(FB, left), :]
-
-    def frames_of(i):
-        return joined[pl.ds(pl.multiple_of(i * FB, FB), FB), :]
-
-    chunks = (count + left) // FB
-    tile(frames_of, chunks, FB, (c0, c1, c2, c3), probs, high, total, (sa, sb))
+    count = line.shape[0]
+    join([(f0, 0), (f1, 0), (line, HELD)], joined, turned)
+    codes = (c0, c1, c2, c3)
+    tile(codes, turned, probs, high, total, (sa, sb), home, arrival)
 
     def put(start, lse):
         lanes = pl.ds(start, lse.shape[1])
@@ -129,7 +133,7 @@
     put(place(1, count), near[:, count:])
     last = merged(high[...], total[...])
     put(place(2, count), last[:, :count])
-    put(pl.multiple_of(place(0, count) + FB, LANES), last[:, count:])
+    put(pl.multiple_of(place(0, count) + HELD, LANES), last[:, count:])
 
 
 def cost_of(count, protos, width):
@@ -140,20 +144,28 @@
     )
 
 
-def tile_call(kernel, tensors, codes, stats, count, last=None):
+def tile_call(kernel, tensors, codes, stats, count, size, last=None):
     width = codes[0].shape[1]
     protos = sum(c.shape[0] for c in codes)
-    blocks = protos // VB
+    blocks = protos // size
     f32, bf16 = jnp.float32, jnp.bfloat16
     stat = jax.ShapeDtypeStruct((blocks, count), f32)
-    scratch = [pltpu.VMEM((VB, FB), f32)] * 2
+    scratch = [
+        pltpu.VMEM((width, count), bf16),
+        pltpu.VMEM((size, count), f32),
+        pltpu.VMEM((size, count), f32),
+        pltpu.VMEM(codes[0].shape, bf16),
+        pltpu.SemaphoreType.DMA,
+    ]
     if len(tensors) > 1:
-        scratch = [pltpu.VMEM((count, width), bf16)] + scratch
+        scratch = scratch + [pltpu.VMEM((count, width), bf16)]
     if last is not None:
         scratch = [pltpu.VMEM((blocks, count), f32)] + scratch
+    home = pl.BlockSpec(memory_space=pltpu.HBM)
+    others = in_vmem(len(codes) - 1 + len(stats))
     return pl.pallas_call(
         kernel,
-        in_specs=in_vmem(len(tensors) + len(codes) + len(stats)),
+        in_specs=in_vmem(len(tensors)) + [home] + others,
         out_specs=in_vmem(3),
         out_shape=[
             jax.ShapeDtypeStruct((protos, count), f32),
@@ -171,7 +183,7 @@
     lse_out, usage_out,
 ):
     count = near_probs.shape[1] // 2
-    left = count - FB
+    left = count - HELD
     groups = near_probs.shape[0] // LANES
     each = groups // 4
     peak = parts[0]
@@ -187,19 +199,20 @@
 
     def hold(probs, high, at, size, start):
         lse = lse_out[:, pl.ds(start, size)]
-        held.append((probs, at, size, jnp.exp(high[:, at : at + size] - lse)))
-
-    hold(own_probs, own_high, 0, FB, place(0, count))
+        weight = jnp.exp(high[:, at : at + size] - lse)
+        held.append((probs, at, size, weight, probs.shape[0] // high.shape[0]))
+
+    hold(own_probs, own_high, 0, HELD, place(0, count))
     hold(near_probs, near_high, 0, count, place(3, count))
     hold(near_probs, near_high, count, count, place(1, count))
     hold(far_probs, far_high, 0, count, place(2, count))
-    rest = pl.multiple_of(place(0, count) + FB, LANES)
+    rest = pl.multiple_of(place(0, count) + HELD, LANES)
     hold(far_probs, far_high, count, left, rest)
 
     for g in range(groups):
-        block = g * LANES // VB
         acc = None
-        for ref, at, size, weight in held:
+        for ref, at, size, weight, each_block in held:
+            block = g * LANES // each_block
             for j in range(0, size, LANES):
                 term = (
                     ref[pl.ds(g * LANES, LANES), pl.ds(at + j, LANES)]
@@ -232,7 +245,7 @@
         cost_estimate=pl.CostEstimate(
             flops=2 * protos * total,
             bytes_accessed=4 * protos * total,
-            transcendentals=total * protos // VB,
+            transcendentals=total * protos // LANES,
         ),
         name="usage_of",
     )(*held, parts)
@@ -268,34 +281,39 @@
     shard_rows, width = own.shape
     owned = codebook.shape[0]
     yh, core = lax.axis_index("yh"), lax.axis_index("core")
-    plane, ring = lax.axis_size(PLANE), lax.axis_size(COLUMN)
+    plane, peers = lax.axis_size(PLANE), lax.axis_size(COLUMN)
     swap = [(0, 1), (1, 0)]
 
-    opposite = lax.ppermute(codebook, RING_Y, [(0, 3), (3, 0), (1, 2), (2, 1)])
+    ring = [(0, 3), (3, 0), (1, 2), (2, 1)]
+    opposite = lax.ppermute(codebook, RING_Y, ring)
     beside = lax.ppermute(codebook, "core", swap)
     line = spread(own, "z").reshape(-1, width)
-    far = shifted(line, 2)
-    before = shifted(line, 1)
-    after = shifted(line, -1)
+    count = line.shape[0]
+    half = count // 2
+    b0 = shifted(line[:half], 1)
+    a1 = shifted(line[half:], -1)
+    b1 = shifted(line[half:], 1)
+    a0 = shifted(line[:half], -1)
     opposite, line = lax.optimization_barrier((opposite, line))
     across = lax.ppermute(opposite, "core", swap)
-
-    count = line.shape[0]
-    codes = (codebook, beside, opposite, across)
+    f0 = shifted(b0, 1)
+    f1 = shifted(a1, -1)
+    home = pltpu.with_memory_space_constraint(codebook, pltpu.HBM)
+    codes = (home, beside, opposite, across)
     own_probs, own_high, own_total = tile_call(
-        own_kernel, (line,), codes, (), FB
+        own_kernel, (line,), codes, (), HELD, 256
     )
     near_probs, near_high, near_total = tile_call(
-        near_kernel, (before, after), codes, (), 2 * count
+        near_kernel, (b0, b1, a0, a1), codes, (), 2 * count, 128
     )
     stats = (own_high, own_total, near_high, near_total)
     far_probs, far_high, part = tile_call(
-        far_kernel, (far, line), codes, stats, 2 * count - FB,
+        far_kernel, (f0, f1, line), codes, stats, 2 * count - HELD, 128,
         (plane, 1, 4 * count),
     )
     parts = exchange(part, PLANE)
     held = (own_probs, own_high, near_probs, near_high, far_probs, far_high)
-    lse, usage = usage_of(held, parts, ring)
+    lse, usage = usage_of(held, parts, peers)
     embeddings = shard_rows * lax.axis_size(BLK) * lax.axis_size("rep")
     column, term = entropy_of(exchange(usage, COLUMN), embeddings, plane)
 

time: 95.8 us -> 93.8 us (0.979)
  waiting for transfers between devices: 27.9 us -> 26.7 us
  local copies, waits for them, and re-layouts: 3.81 us -> 2.72 us
    ppermute x3 -> x6, starting transfers between devices: 4.21 us -> 7.91 us  [shifted(): return lax.ppermute(array, 'x', [(i, (i + step) % n) for i in range(n)])]
    all_to_all x3, starting transfers between devices: 23.7 us -> 20.3 us  [exchange(): return lax.all_to_all(array, axis, split_axis=0, concat_axis=0, tiled=True)]
    ppermute x3 -> x6, waiting for transfers between devices: 5.82 us -> 4.63 us  [shifted(): return lax.ppermute(array, 'x', [(i, (i + step) % n) for i in range(n)])]
    unnamed x2 -> x0, local copies, waits for them, and re-layouts: 1.13 us -> none
  transfers between devices with their start and end apart: 9 -> 12, of which waited for: 5 -> 5; matrix products, arithmetic and copies ran while one was open for 3% -> 3% of each run, Pallas kernels for 6% -> 6%
where the time goes in v3:
time: 93.8 us; the launch traced here: 93.3 us
  starting transfers between devices  35.9 us (38%)
  waiting for transfers between devices  26.7 us (28%)
  blocking collectives  13.6 us (14%)
  Pallas kernels  13.1 us (14%)
  local copies, waits for them, and re-layouts  2.72 us (3%)
    all_to_all x3, waiting for transfers between devices, exchange(): return lax.all_to_all(array, axis, split_axis=0, concat_axis=0, tiled=True)  22.1 us
    all_to_all x3, starting transfers between devices, exchange(): return lax.all_to_all(array, axis, split_axis=0, concat_axis=0, tiled=True)  20.3 us
    all_to_all x1, blocking collectives, exchange(): return lax.all_to_all(array, axis, split_axis=0, concat_axis=0, tiled=True)  13.6 us
    pallas_call x3, Pallas kernels, tile_call(): pl.pallas_call(kernel, in_specs=in_vmem(len(tensors)) + [home] + others,...  9.54 us
    ppermute x6, starting transfers between devices, shifted(): return lax.ppermute(array, 'x', [(i, (i + step) % n) for i in range(n)])  7.91 us
    ppermute x6, waiting for transfers between devices, shifted(): return lax.ppermute(array, 'x', [(i, (i + step) % n) for i in range(n)])  4.63 us
    ppermute x1, starting transfers between devices, per_device(): opposite = lax.ppermute(codebook, RING_Y, ring)  3.64 us
    pallas_call x1, Pallas kernels, usage_of(): pl.pallas_call(usage_kernel, in_specs=in_vmem(len(held) + 1), out_specs=i...  2.78 us
  transfers between devices with their start and end apart: 12, of which 5 were waited for; matrix products, arithmetic and copies ran while one was open for 3% of the time, Pallas kernels for 6%

profile of v3, /device:TPU:1, one launch (start us, length us, event | category | flops | bytes accessed | tf_op | source)
XLA Modules:
  0.0 93.3 jit_solution(17197780910635861610)
XLA Ops:
  0.6 3.6 %collective-permute-start = (bf16[1024,384]{1,0:T(8,128)(2,1)}, bf16[1024,384]{1,0:T(8,128)(2,1)S(1)}, u32[]{:S(2)}, u32[]{:S(2)}) collective-permute-start(bf16[1024,384]{1,0:T(8,128)(2,1)} %c0.5), channel_id=1, source_target_pairs={{0,5},{5,0},{1,4},{4,1},{2,7},{7,2},{3,6},{6,3},{8,13},{13,8},{9,1... | collective-permute-start | bytes 2359304 | tf_op jit(solution)/shard_map/ppermute | solution.py:288
  4.3 1.5 %broadcast_in_dim.3 = bf16[8,48,384]{2,1,0:T(8,128)(2,1)} broadcast(bf16[48,384]{1,0:T(8,128)(2,1)} %bitcast.12), dimensions={1,2} | broadcast | bytes 331776 | tf_op jit(solution)/shard_map/broadcast_in_dim | solution.py:27
  5.8 8.2 %all-to-all-start = ((bf16[8,48,384]{2,1,0:T(8,128)(2,1)}), bf16[8,48,384]{2,1,0:T(8,128)(2,1)S(1)}, u32[]{:S(2)}, u32[]{:S(2)}) async-start(bf16[8,48,384]{2,1,0:T(8,128)(2,1)} %broadcast_in_dim.3), calls=%async_computation | async-start | bytes 589824 | tf_op jit(solution)/shard_map/all_to_all | solution.py:22
  14.0 1.2 %collective-permute-start.1 = (bf16[1024,384]{1,0:T(8,128)(2,1)}, bf16[1024,384]{1,0:T(8,128)(2,1)S(1)}, u32[]{:S(2)}, u32[]{:S(2)}) collective-permute-start(bf16[1024,384]{1,0:T(8,128)(2,1)} %c0.5), channel_id=1, source_target_pairs={{0,2},{2,0},{1,3},{3,1},{4,6},{6,4},{5,7},{7,5},{8,10},{10,8},{9,1... | collective-permute-start | bytes 2359304 | tf_op jit(solution)/shard_map/ppermute | solution.py:289
  15.2 9.6 %all-to-all-done = bf16[8,48,384]{2,1,0:T(8,128)(2,1)S(1)} async-done(((bf16[8,48,384]{2,1,0:T(8,128)(2,1)}), bf16[8,48,384]{2,1,0:T(8,128)(2,1)S(1)}, u32[]{:S(2)}, u32[]{:S(2)}) %all-to-all-start) | async-done | bytes 294944 | tf_op jit(solution)/shard_map/all_to_all | solution.py:22
  24.7 0.0 collective-permute-done.c2
  24.7 2.7 %collective-permute-start.2 = (bf16[1024,384]{1,0:T(8,128)(2,1)S(1)}, bf16[1024,384]{1,0:T(8,128)(2,1)S(1)}, u32[]{:S(2)}, u32[]{:S(2)}) collective-permute-start(bf16[1024,384]{1,0:T(8,128)(2,1)S(1)} %collective-permute-done.c2), channel_id=1, source_target_pairs={{0,2},{2,0},{1,3},{3,1},{4,6},{6,4},{5,7},{7,5},{8,10},{10,8},{9,1... | collective-permute-start | bytes 2359304 | tf_op jit(solution)/shard_map/ppermute | solution.py:298
  27.5 1.3 %collective-permute-start.3 = (bf16[192,384]{1,0:T(8,128)(2,1)S(1)}, bf16[192,384]{1,0:T(8,128)(2,1)S(1)}, u32[]{:S(2)}, u32[]{:S(2)}) collective-permute-start(bf16[192,384]{1,0:T(8,128)(2,1)S(1)} %bitcast.8), channel_id=1, source_target_pairs={{0,64},{64,128},{128,192},{192,0},{1,65},{65,129},{129,193},{193,1... | collective-permute-start | bytes 442376 | tf_op jit(solution)/shard_map/ppermute | solution.py:32
  28.8 1.2 %collective-permute-start.4 = (bf16[192,384]{1,0:T(8,128)(2,1)S(1)}, bf16[192,384]{1,0:T(8,128)(2,1)S(1)}, u32[]{:S(2)}, u32[]{:S(2)}) collective-permute-start(bf16[192,384]{1,0:T(8,128)(2,1)S(1)} %bitcast.10), channel_id=1, source_target_pairs={{0,64},{64,128},{128,192},{192,0},{1,65},{65,129},{129,193},{193,1... | collective-permute-start | bytes 442376 | tf_op jit(solution)/shard_map/ppermute | solution.py:32
  30.0 1.5 %collective-permute-start.6 = (bf16[192,384]{1,0:T(8,128)(2,1)S(1)}, bf16[192,384]{1,0:T(8,128)(2,1)S(1)}, u32[]{:S(2)}, u32[]{:S(2)}) collective-permute-start(bf16[192,384]{1,0:T(8,128)(2,1)S(1)} %bitcast.11), channel_id=1, source_target_pairs={{0,192},{64,0},{128,64},{192,128},{1,193},{65,1},{129,65},{193,129... | collective-permute-start | bytes 442376 | tf_op jit(solution)/shard_map/ppermute | solution.py:32
  31.5 2.7 %collective-permute-done.3.b0 = bf16[192,384]{1,0:T(8,128)(2,1)S(1)} collective-permute-done((bf16[192,384]{1,0:T(8,128)(2,1)S(1)}, bf16[192,384]{1,0:T(8,128)(2,1)S(1)}, u32[]{:S(2)}, u32[]{:S(2)}) %collective-permute-start.3) | collective-permute-done | bytes 147488 | tf_op jit(solution)/shard_map/ppermute | solution.py:32
  34.2 1.3 %collective-permute-start.5 = (bf16[192,384]{1,0:T(8,128)(2,1)S(1)}, bf16[192,384]{1,0:T(8,128)(2,1)S(1)}, u32[]{:S(2)}, u32[]{:S(2)}) collective-permute-start(bf16[192,384]{1,0:T(8,128)(2,1)S(1)} %bitcast.9), channel_id=1, source_target_pairs={{0,192},{64,0},{128,64},{192,128},{1,193},{65,1},{129,65},{193,129... | collective-permute-start | bytes 442376 | tf_op jit(solution)/shard_map/ppermute | solution.py:32
  35.5 1.9 %collective-permute-done.4.b1 = bf16[192,384]{1,0:T(8,128)(2,1)S(1)} collective-permute-done((bf16[192,384]{1,0:T(8,128)(2,1)S(1)}, bf16[192,384]{1,0:T(8,128)(2,1)S(1)}, u32[]{:S(2)}, u32[]{:S(2)}) %collective-permute-start.4) | collective-permute-done | bytes 147488 | tf_op jit(solution)/shard_map/ppermute | solution.py:32
  37.4 0.0 collective-permute-start.7
  37.4 0.0 collective-permute-done.6.a1
  37.4 2.7 %collective-permute-start.8 = (bf16[192,384]{1,0:T(8,128)(2,1)S(1)}, bf16[192,384]{1,0:T(8,128)(2,1)S(1)}, u32[]{:S(2)}, u32[]{:S(2)}) collective-permute-start(bf16[192,384]{1,0:T(8,128)(2,1)S(1)} %collective-permute-done.6.a1), channel_id=1, source_target_pairs={{0,192},{64,0},{128,64},{192,128},{1,193},{65,1},{129,65},{193,129... | collective-permute-start | bytes 442376 | tf_op jit(solution)/shard_map/ppermute | solution.py:32
  40.1 0.0 collective-permute-done.5.a0
  40.1 0.0 collective-permute-done.1.c1
  40.1 0.0 collective-permute-done.2.c3
  40.1 3.9 %shard_map.50 = (f32[4096,768]{1,0:T(8,128)S(1)}, f32[32,768]{1,0:T(8,128)S(1)}, f32[32,768]{1,0:T(8,128)S(1)}) custom-call(bf16[192,384]{1,0:T(8,128)(2,1)S(1)} %collective-permute-done.3.b0, bf16[192,384]{1,0:T(8,128)(2,1)S(1)} %collective-permute-done.4.b1, bf16[192,384]{1,0:T(8,128)(2,1)S(1)} %collective-permute-done.5.a0, ...), custom_call_target="tpu_custom_call" | custom-call | flops 2415919104 | bytes 12582912 | tf_op jit(solution)/shard_map/pallas_call | solution.py:166
  44.0 1.7 %shard_map.49 = (f32[4096,256]{1,0:T(8,128)S(1)}, f32[16,256]{1,0:T(8,128)S(1)}, f32[16,256]{1,0:T(8,128)S(1)}) custom-call(bf16[384,384]{1,0:T(8,128)(2,1)S(1)} %bitcast.6, bf16[1024,384]{1,0:T(8,128)(2,1)} %c0.5, bf16[1024,384]{1,0:T(8,128)(2,1)S(1)} %collective-permute-done.1.c1, bf16[1024,384]{1,0:T(8,128)(2,1)S(1)} %collective-permute-done.c2, ...), custom_call_target="tpu_custom_call" | custom-call | flops 805306368 | bytes 4194304 | tf_op jit(solution)/shard_map/pallas_call | solution.py:166
  45.7 0.0 collective-permute-done.7.f0
  45.7 0.0 collective-permute-done.8.f1
  45.7 3.9 %shard_map.51 = (f32[4096,512]{1,0:T(8,128)S(1)}, f32[32,512]{1,0:T(8,128)S(1)}, f32[32,1,1536]{2,1,0:T(1,128)S(1)}) custom-call(bf16[192,384]{1,0:T(8,128)(2,1)S(1)} %collective-permute-done.7.f0, bf16[192,384]{1,0:T(8,128)(2,1)S(1)} %collective-permute-done.8.f1, bf16[384,384]{1,0:T(8,128)(2,1)S(1)} %bitcast.7, bf16[1024,384]{1,0:T(8,128)(2,1)} %c0.5, ...), custom_call_target="tpu_custom_call" | custom-call | flops 1610612736 | bytes 8388608 | tf_op jit(solution)/shard_map/pallas_call | solution.py:166
  49.7 13.6 %all_to_all.20.parts = f32[32,1,1536]{2,1,0:T(1,128)S(1)} all-to-all(f32[32,1,1536]{2,1,0:T(1,128)S(1)} %get-tuple-element.28), channel_id=1, replica_groups=mesh['x'=4,'z'=8,'yh'=2,'core'=2,'rep'=2] {'x','z'}, dimensions={0} | all-to-all | bytes 393216 | tf_op jit(solution)/shard_map/all_to_all | solution.py:22
  63.2 2.8 %usage_of.1 = (f32[1,1536]{1,0:T(1,128)S(1)}, f32[8,32,128]{2,1,0:T(8,128)}) custom-call(f32[4096,256]{1,0:T(8,128)S(1)} %get-tuple-element.20.own_probs, f32[16,256]{1,0:T(8,128)S(1)} %get-tuple-element.21.own_high, f32[4096,768]{1,0:T(8,128)S(1)} %get-tuple-element.22.near_probs, f32[32,768]{1,0:T(8,128)S(1)} %get-tuple-element.23.near_high, ...), custom_call_target="tpu_custom_call" | custom-call | flops 12582912 | bytes 25165824 | tf_op jit(solution)/shard_map/usage_of/pallas_call | solution.py:236
  66.0 8.3 %all-to-all-start.2 = ((f32[8,32,128]{2,1,0:T(8,128)}), f32[8,32,128]{2,1,0:T(8,128)S(1)}, u32[]{:S(2)}, u32[]{:S(2)}) async-start(f32[8,32,128]{2,1,0:T(8,128)} %get-tuple-element.30), calls=%async_computation.2 | async-start | bytes 262144 | tf_op jit(solution)/shard_map/all_to_all | solution.py:22
  74.3 0.6 constant_dynamic-slice_fusion
  74.9 4.5 %all-to-all-done.2.counts = f32[8,32,128]{2,1,0:T(8,128)S(1)} async-done(((f32[8,32,128]{2,1,0:T(8,128)}), f32[8,32,128]{2,1,0:T(8,128)S(1)}, u32[]{:S(2)}, u32[]{:S(2)}) %all-to-all-start.2) | async-done | bytes 131104 | tf_op jit(solution)/shard_map/all_to_all | solution.py:22
  79.4 0.7 entropy_of.1
  80.1 3.8 %all-to-all-start.3 = ((f32[32,1,128]{2,1,0:T(1,128)}), f32[32,1,128]{2,1,0:T(1,128)S(1)}, u32[]{:S(2)}, u32[]{:S(2)}) async-start(f32[32,1,128]{2,1,0:T(1,128)} %get-tuple-element.32), calls=%async_computation.3 | async-start | bytes 32768 | tf_op jit(solution)/shard_map/all_to_all | solution.py:22
  84.0 0.6 dynamic-slice_bitcast_fusion
  84.6 8.0 %all-to-all-done.3 = f32[32,1,128]{2,1,0:T(1,128)S(1)} async-done(((f32[32,1,128]{2,1,0:T(1,128)}), f32[32,1,128]{2,1,0:T(1,128)S(1)}, u32[]{:S(2)}, u32[]{:S(2)}) %all-to-all-start.3) | async-done | bytes 16416 | tf_op jit(solution)/shard_map/all_to_all | solution.py:22
  92.6 0.6 slice_reduce_fusion
  (1 shorter events, 0.0 us)
Async XLA Ops:
  0.6 24.1 %collective-permute-start = (bf16[1024,384]{1,0:T(8,128)(2,1)}, bf16[1024,384]{1,0:T(8,128)(2,1)S(1)}, u32[]{:S(2)}, u32[]{:S(2)}) collective-permute-start(bf16[1024,384]{1,0:T(8,128)(2,1)} %c0.5), channel_id=1, source_target_pairs={{0,5},{5,0},{1,4},{4,1},{2,7},{7,2},{3,6},{6,3},{8,13},{13,8},{9,1... | collective-permute-start | bytes 2359304 | tf_op jit(solution)/shard_map/ppermute | solution.py:288
  5.8 19.0 %all-to-all-start = ((bf16[8,48,384]{2,1,0:T(8,128)(2,1)}), bf16[8,48,384]{2,1,0:T(8,128)(2,1)S(1)}, u32[]{:S(2)}, u32[]{:S(2)}) async-start(bf16[8,48,384]{2,1,0:T(8,128)(2,1)} %broadcast_in_dim.3), calls=%async_computation | async-start | bytes 589824 | tf_op jit(solution)/shard_map/all_to_all | solution.py:22
  14.0 26.1 %collective-permute-start.1 = (bf16[1024,384]{1,0:T(8,128)(2,1)}, bf16[1024,384]{1,0:T(8,128)(2,1)S(1)}, u32[]{:S(2)}, u32[]{:S(2)}) collective-permute-start(bf16[1024,384]{1,0:T(8,128)(2,1)} %c0.5), channel_id=1, source_target_pairs={{0,2},{2,0},{1,3},{3,1},{4,6},{6,4},{5,7},{7,5},{8,10},{10,8},{9,1... | collective-permute-start | bytes 2359304 | tf_op jit(solution)/shard_map/ppermute | solution.py:289
  24.7 15.3 %collective-permute-start.2 = (bf16[1024,384]{1,0:T(8,128)(2,1)S(1)}, bf16[1024,384]{1,0:T(8,128)(2,1)S(1)}, u32[]{:S(2)}, u32[]{:S(2)}) collective-permute-start(bf16[1024,384]{1,0:T(8,128)(2,1)S(1)} %collective-permute-done.c2), channel_id=1, source_target_pairs={{0,2},{2,0},{1,3},{3,1},{4,6},{6,4},{5,7},{7,5},{8,10},{10,8},{9,1... | collective-permute-start | bytes 2359304 | tf_op jit(solution)/shard_map/ppermute | solution.py:298
  27.5 6.7 %collective-permute-start.3 = (bf16[192,384]{1,0:T(8,128)(2,1)S(1)}, bf16[192,384]{1,0:T(8,128)(2,1)S(1)}, u32[]{:S(2)}, u32[]{:S(2)}) collective-permute-start(bf16[192,384]{1,0:T(8,128)(2,1)S(1)} %bitcast.8), channel_id=1, source_target_pairs={{0,64},{64,128},{128,192},{192,0},{1,65},{65,129},{129,193},{193,1... | collective-permute-start | bytes 442376 | tf_op jit(solution)/shard_map/ppermute | solution.py:32
  28.8 8.6 %collective-permute-start.4 = (bf16[192,384]{1,0:T(8,128)(2,1)S(1)}, bf16[192,384]{1,0:T(8,128)(2,1)S(1)}, u32[]{:S(2)}, u32[]{:S(2)}) collective-permute-start(bf16[192,384]{1,0:T(8,128)(2,1)S(1)} %bitcast.10), channel_id=1, source_target_pairs={{0,64},{64,128},{128,192},{192,0},{1,65},{65,129},{129,193},{193,1... | collective-permute-start | bytes 442376 | tf_op jit(solution)/shard_map/ppermute | solution.py:32
  30.0 7.4 %collective-permute-start.6 = (bf16[192,384]{1,0:T(8,128)(2,1)S(1)}, bf16[192,384]{1,0:T(8,128)(2,1)S(1)}, u32[]{:S(2)}, u32[]{:S(2)}) collective-permute-start(bf16[192,384]{1,0:T(8,128)(2,1)S(1)} %bitcast.11), channel_id=1, source_target_pairs={{0,192},{64,0},{128,64},{192,128},{1,193},{65,1},{129,65},{193,129... | collective-permute-start | bytes 442376 | tf_op jit(solution)/shard_map/ppermute | solution.py:32
  34.2 5.8 %collective-permute-start.5 = (bf16[192,384]{1,0:T(8,128)(2,1)S(1)}, bf16[192,384]{1,0:T(8,128)(2,1)S(1)}, u32[]{:S(2)}, u32[]{:S(2)}) collective-permute-start(bf16[192,384]{1,0:T(8,128)(2,1)S(1)} %bitcast.9), channel_id=1, source_target_pairs={{0,192},{64,0},{128,64},{192,128},{1,193},{65,1},{129,65},{193,129... | collective-permute-start | bytes 442376 | tf_op jit(solution)/shard_map/ppermute | solution.py:32
  37.4 8.3 %collective-permute-start.7 = (bf16[192,384]{1,0:T(8,128)(2,1)S(1)}, bf16[192,384]{1,0:T(8,128)(2,1)S(1)}, u32[]{:S(2)}, u32[]{:S(2)}) collective-permute-start(bf16[192,384]{1,0:T(8,128)(2,1)S(1)} %collective-permute-done.3.b0), channel_id=1, source_target_pairs={{0,64},{64,128},{128,192},{192,0},{1,65},{65,129},{129,193},{193,1... | collective-permute-start | bytes 442376 | tf_op jit(solution)/shard_map/ppermute | solution.py:32
  37.4 8.3 %collective-permute-start.8 = (bf16[192,384]{1,0:T(8,128)(2,1)S(1)}, bf16[192,384]{1,0:T(8,128)(2,1)S(1)}, u32[]{:S(2)}, u32[]{:S(2)}) collective-permute-start(bf16[192,384]{1,0:T(8,128)(2,1)S(1)} %collective-permute-done.6.a1), channel_id=1, source_target_pairs={{0,192},{64,0},{128,64},{192,128},{1,193},{65,1},{129,65},{193,129... | collective-permute-start | bytes 442376 | tf_op jit(solution)/shard_map/ppermute | solution.py:32
  66.0 13.4 %all-to-all-start.2 = ((f32[8,32,128]{2,1,0:T(8,128)}), f32[8,32,128]{2,1,0:T(8,128)S(1)}, u32[]{:S(2)}, u32[]{:S(2)}) async-start(f32[8,32,128]{2,1,0:T(8,128)} %get-tuple-element.30), calls=%async_computation.2 | async-start | bytes 262144 | tf_op jit(solution)/shard_map/all_to_all | solution.py:22
  80.1 12.5 %all-to-all-start.3 = ((f32[32,1,128]{2,1,0:T(1,128)}), f32[32,1,128]{2,1,0:T(1,128)S(1)}, u32[]{:S(2)}, u32[]{:S(2)}) async-start(f32[32,1,128]{2,1,0:T(1,128)} %get-tuple-element.32), calls=%async_computation.3 | async-start | bytes 32768 | tf_op jit(solution)/shard_map/all_to_all | solution.py:22

commit v4 on v3

v4 whole, which is shorter than its diff:
```python
import functools

import jax
import jax.numpy as jnp
from jax import lax
from jax.experimental import pallas as pl
from jax.experimental.pallas import tpu as pltpu
from jax.sharding import Mesh
from jax.sharding import PartitionSpec as P


BLK = ("x", "z", "yh", "core")
RING_Y = ("yh", "rep")
COLUMN = ("yh", "core", "rep")
PLANE = ("x", "z")
LOG2E = 1.4426950408889634
HELD = 256
LANES = 128


def exchange(array, axis):
    return lax.all_to_all(array, axis, split_axis=0, concat_axis=0, tiled=True)


def spread(array, axis):
    n = lax.axis_size(axis)
    return exchange(jnp.broadcast_to(array, (n, *array.shape)), axis)


def shifted(array, step):
    n = lax.axis_size("x")
    return lax.ppermute(array, "x", [(i, (i + step) % n) for i in range(n)])


def in_vmem(count):
    return [pl.BlockSpec(memory_space=pltpu.VMEM)] * count


def scores_into(scratch, codes, start, turned):
    s = jnp.dot(
        codes[pl.ds(start, scratch.shape[0]), :],
        turned[...],
        preferred_element_type=jnp.float32,
    )
    scratch[:, pl.ds(0, turned.shape[1])] = s
    return jnp.max(s, axis=0, keepdims=True)


def tile(codes, turned, probs, high, total, scratch, home, arrival):
    fetch = pltpu.make_async_copy(codes[0], home, arrival)
    fetch.start()
    size = scratch[0].shape[0]
    steps = [
        (slot, start)
        for slot in (1, 2, 3, 0)
        for start in range(0, codes[slot].shape[0], size)
    ]

    def scores_at(k):
        slot, start = steps[k]
        if slot == 0 and start == 0:
            fetch.wait()
        ref = home if slot == 0 else codes[slot]
        return scores_into(scratch[k % 2], ref, start, turned)

    top = scores_at(0)
    for k in range(len(steps)):
        later = scores_at(k + 1) if k + 1 < len(steps) else None
        slot, start = steps[k]
        at = slot * home.shape[0] + start
        p = jnp.exp2((scratch[k % 2][:, pl.ds(0, probs.shape[1])] - top) * LOG2E)
        probs[pl.ds(at, size), :] = p
        high[pl.ds(at // size, 1), :] = top
        total[pl.ds(at // size, 1), :] = jnp.sum(p, axis=0, keepdims=True)
        top = later


def merged(high, total):
    top = jnp.max(high, axis=0, keepdims=True)
    return top + jnp.log(
        jnp.sum(total * jnp.exp(high - top), axis=0, keepdims=True)
    )


def turned_kernel(line, out):
    out[...] = line[pl.ds(0, out.shape[1]), :].T


def turned_of(line, count):
    return pl.pallas_call(
        turned_kernel,
        in_specs=in_vmem(1),
        out_specs=in_vmem(1)[0],
        out_shape=jax.ShapeDtypeStruct((line.shape[1], count), line.dtype),
        compiler_params=pltpu.CompilerParams(vmem_limit_bytes=4 * 1024 * 1024),
        name="turned_of",
    )(line)


def own_kernel(
    line, c0, c1, c2, c3, probs, high, total, turned, sa, sb, home, arrival
):
    turned[...] = line[...]
    codes = (c0, c1, c2, c3)
    tile(codes, turned, probs, high, total, (sa, sb), home, arrival)


def join(pieces, joined):
    at = 0
    for ref in pieces:
        joined[pl.ds(at, ref.shape[0]), :] = ref[...]
        at += ref.shape[0]


def near_kernel(
    b0, b1, a0, a1, c0, c1, c2, c3, probs, high, total,
    turned, sa, sb, home, arrival, joined,
):
    join((b0, b1, a0, a1), joined)
    turned[...] = joined[...].T
    codes = (c0, c1, c2, c3)
    tile(codes, turned, probs, high, total, (sa, sb), home, arrival)


def place(line, rows):
    return lax.rem(lax.axis_index("x") + line, lax.axis_size("x")) * rows


def far_kernel(
    f0, f1, line, c0, c1, c2, c3, own_high, own_total, near_high, near_total,
    probs, high, lse_out, dense, total, turned, sa, sb, home, arrival, joined,
):
    count = line.shape[0]
    join((f0, f1), joined)
    turned[:, pl.ds(0, count)] = joined[...].T
    turned[:, pl.ds(count, count - HELD)] = line[pl.ds(HELD, count - HELD), :].T
    codes = (c0, c1, c2, c3)
    tile(codes, turned, probs, high, total, (sa, sb), home, arrival)

    rows = count // LANES

    def put(row, lse):
        for j in range(lse.shape[1] // LANES):
            dense[pl.ds(row + j, 1), :] = lse[:, j * LANES : (j + 1) * LANES]

    put(place(0, rows), merged(own_high[...], own_total[...]))
    near = merged(near_high[...], near_total[...])
    put(place(3, rows), near[:, :count])
    put(place(1, rows), near[:, count:])
    last = merged(high[...], total[...])
    put(place(2, rows), last[:, :count])
    put(place(0, rows) + HELD // LANES, last[:, count:])
    lse = dense[...]
    twice = jnp.concatenate([lse, lse])
    step = twice.shape[0]
    for k in range(lse_out.shape[0] // step):
        lse_out[pl.ds(k * step, step), :] = twice


def cost_of(count, protos, width):
    return pl.CostEstimate(
        flops=2 * count * protos * width,
        bytes_accessed=4 * count * protos,
        transcendentals=count * protos,
    )


def tile_call(kernel, tensors, codes, stats, count, size, last=None):
    width = codes[0].shape[1]
    protos = sum(c.shape[0] for c in codes)
    blocks = protos // size
    f32, bf16 = jnp.float32, jnp.bfloat16
    stat = jax.ShapeDtypeStruct((blocks, count), f32)
    scratch = [
        pltpu.VMEM((size, count + LANES), f32),
        pltpu.VMEM((size, count + LANES), f32),
        pltpu.VMEM(codes[0].shape, bf16),
        pltpu.SemaphoreType.DMA,
    ]
    turned = pltpu.VMEM((width, count), bf16)
    scratch = [turned] + scratch
    if len(tensors) > 1:
        pieces = tensors if last is None else tensors[:2]
        held = sum(t.shape[0] for t in pieces)
        scratch = scratch + [pltpu.VMEM((held, width), bf16)]
    if last is not None:
        dense = pltpu.VMEM((last[0] // lax.axis_size(PLANE), LANES), f32)
        scratch = [dense, pltpu.VMEM((blocks, count), f32)] + scratch
    home = pl.BlockSpec(memory_space=pltpu.HBM)
    others = in_vmem(len(codes) - 1 + len(stats))
    return pl.pallas_call(
        kernel,
        in_specs=in_vmem(len(tensors)) + [home] + others,
        out_specs=in_vmem(3),
        out_shape=[
            jax.ShapeDtypeStruct((protos, count), f32),
            stat,
            stat if last is None else jax.ShapeDtypeStruct(last, f32),
        ],
        scratch_shapes=scratch,
        compiler_params=pltpu.CompilerParams(vmem_limit_bytes=8 * 1024 * 1024),
        cost_estimate=cost_of(count, protos, width),
    )(*tensors, *codes, *stats)


def usage_kernel(
    own_probs, own_high, near_probs, near_high, far_probs, far_high, parts,
    own_out, usage_out, lse_out, column,
):
    count = near_probs.shape[1] // 2
    left = count - HELD
    groups = near_probs.shape[0] // LANES
    each = groups // 4
    rows = count // LANES
    lines = lse_out.shape[0]
    pairs = range(0, parts.shape[0], 2 * lines)

    def both(combine, pair):
        return combine(pair[:lines], pair[lines:])

    peak = parts[pl.ds(0, 2 * lines), :]
    for k in pairs[1:]:
        peak = jnp.maximum(peak, parts[pl.ds(k, 2 * lines), :])
    peak = both(jnp.maximum, peak)
    twice = jnp.concatenate([peak, peak])
    mass = jnp.exp(parts[pl.ds(0, 2 * lines), :] - twice)
    for k in pairs[1:]:
        mass = mass + jnp.exp(parts[pl.ds(k, 2 * lines), :] - twice)
    lse_out[...] = peak + jnp.log(both(jnp.add, mass))

    shown = own_out.shape[1]
    at = lax.axis_index(PLANE) * shown
    row, shift = at // LANES, lax.rem(LANES - lax.rem(at, LANES), LANES)
    first = pltpu.roll(lse_out[pl.ds(row, 1), :], shift, 1)
    second = lse_out[pl.ds(jnp.minimum(row + 1, lines - 1), 1), :]
    second = pltpu.roll(second, shift, 1)
    lane = lax.broadcasted_iota(jnp.int32, (1, LANES), 1)
    straddle = jnp.logical_and(shift > 0, lane >= shift)
    own_out[...] = jnp.where(straddle, second, first)[:, :shown]

    yh, core = lax.axis_index("yh"), lax.axis_index("core")
    held = []

    def hold(probs, high, at, size, row):
        block = probs.shape[0] // high.shape[0]
        for j in range(0, size, LANES):
            lse = lse_out[pl.ds(row + j // LANES, 1), :]
            weight = jnp.exp(high[:, at + j : at + j + LANES] - lse)
            held.append((probs, at + j, weight, block))

    hold(own_probs, own_high, 0, HELD, place(0, rows))
    hold(near_probs, near_high, 0, count, place(3, rows))
    hold(near_probs, near_high, count, count, place(1, rows))
    hold(far_probs, far_high, 0, count, place(2, rows))
    hold(far_probs, far_high, count, left, place(0, rows) + HELD // LANES)

    for g in range(groups):
        acc = None
        for ref, at, weight, size in held:
            block = g * LANES // size
            row = jnp.broadcast_to(weight[block : block + 1, :], (8, LANES))
            probs = ref[pl.ds(g * LANES, LANES), pl.ds(at, LANES)]
            term = probs.reshape(-1, 8, LANES) * row
            acc = term if acc is None else acc + term
        acc = acc.reshape(LANES, LANES)
        line = jnp.sum(acc.T, axis=0, keepdims=True)
        flip = g // each
        far, beside = flip // 2, flip % 2
        owner = jnp.where(yh == 1, 2 - 2 * far, 2 * far) + jnp.where(
            core == 1, 1 - beside, beside
        )
        column[pl.ds(owner * each + g % each, 1), :] = line
    for k in range(usage_out.shape[0]):
        usage_out[k] = column[...]


def usage_of(held, parts, copies, shown):
    protos = held[0].shape[0]
    total = parts.shape[0] * LANES // lax.axis_size(PLANE)
    f32 = jnp.float32
    return pl.pallas_call(
        usage_kernel,
        in_specs=in_vmem(len(held) + 1),
        out_specs=in_vmem(2),
        out_shape=[
            jax.ShapeDtypeStruct((1, shown), f32),
            jax.ShapeDtypeStruct((copies, protos // LANES, LANES), f32),
        ],
        scratch_shapes=[
            pltpu.VMEM((total // LANES, LANES), f32),
            pltpu.VMEM((protos // LANES, LANES), f32),
        ],
        compiler_params=pltpu.CompilerParams(vmem_limit_bytes=8 * 1024 * 1024),
        cost_estimate=pl.CostEstimate(
            flops=2 * protos * total,
            bytes_accessed=4 * protos * total,
            transcendentals=total * protos // LANES,
        ),
        name="usage_of",
    )(*held, parts)


def entropy_kernel(embeddings, counts, own_out, term_out, column_out):
    column = counts[0]
    for k in range(1, counts.shape[0]):
        column = column + counts[k]
    column_out[...] = column
    slot = 2 * lax.axis_index("yh") + lax.axis_index("core")
    rows = own_out.shape[0]
    own_out[...] = column_out[pl.ds(pl.multiple_of(slot * rows, rows), rows), :]
    mean_use = column / embeddings
    term = -jnp.sum(mean_use * jnp.log(mean_use + 1e-07), keepdims=True)
    term_out[...] = jnp.broadcast_to(term[None], term_out.shape)


def entropy_of(counts, embeddings, copies):
    f32 = jnp.float32
    return pl.pallas_call(
        functools.partial(entropy_kernel, embeddings),
        in_specs=in_vmem(1),
        out_specs=in_vmem(2),
        out_shape=[
            jax.ShapeDtypeStruct((counts.shape[1] // 4, LANES), f32),
            jax.ShapeDtypeStruct((copies, 1, LANES), f32),
        ],
        scratch_shapes=[pltpu.VMEM(counts.shape[1:], f32)],
        compiler_params=pltpu.CompilerParams(vmem_limit_bytes=4 * 1024 * 1024),
        name="entropy_of",
    )(counts)


def per_device(frames, codebook):
    own = frames[0]
    shard_rows, width = own.shape
    owned = codebook.shape[0]
    plane, peers = lax.axis_size(PLANE), lax.axis_size(COLUMN)
    swap = [(0, 1), (1, 0)]

    ring = [(0, 3), (3, 0), (1, 2), (2, 1)]
    opposite = lax.ppermute(codebook, RING_Y, ring)
    beside = lax.ppermute(codebook, "core", swap)
    line = spread(own, "z").reshape(-1, width)
    count = line.shape[0]
    half = count // 2
    b0 = shifted(line[:half], 1)
    a1 = shifted(line[half:], -1)
    b1 = shifted(line[half:], 1)
    a0 = shifted(line[:half], -1)
    opposite, line = lax.optimization_barrier((opposite, line))
    across = lax.ppermute(opposite, "core", swap)
    f0 = shifted(b0, 1)
    f1 = shifted(a1, -1)
    home = pltpu.with_memory_space_constraint(codebook, pltpu.HBM)
    codes = (home, beside, opposite, across)
    turned = turned_of(line, HELD)
    own_probs, own_high, own_total = tile_call(
        own_kernel, (turned,), codes, (), HELD, 256
    )
    near_probs, near_high, near_total = tile_call(
        near_kernel, (b0, b1, a0, a1), codes, (), 2 * count, 128
    )
    stats = (own_high, own_total, near_high, near_total)
    far_probs, far_high, part = tile_call(
        far_kernel, (f0, f1, line), codes, stats, 2 * count - HELD, 128,
        (plane * 4 * count // LANES, LANES),
    )
    parts = exchange(part.reshape(plane, 1, 4 * count), PLANE).reshape(part.shape)
    held = (own_probs, own_high, near_probs, near_high, far_probs, far_high)
    lse_own, usage = usage_of(held, parts, peers, shard_rows)
    embeddings = shard_rows * lax.axis_size(BLK) * lax.axis_size("rep")
    usage_own, term = entropy_of(exchange(usage, COLUMN), embeddings, plane)
    entropy = jnp.sum(exchange(term, PLANE)[:, 0, 0])
    return (lse_own, usage_own.reshape(owned), entropy)


def solution(mesh):
    split = Mesh(
        mesh.devices.reshape(4, 8, 2, 2, mesh.shape["rep"]),
        ("x", "z", "yh", "core", "rep"),
    )
    return jax.shard_map(
        per_device,
        mesh=split,
        in_specs=(P("rep", BLK, None), P(BLK, None)),
        out_specs=(P("rep", BLK), P(BLK), P()),
        check_vma=False,
    )
```

time: 93.8 us -> 93 us (level)
  blocking collectives: 13.6 us -> 40.7 us
  waiting for transfers between devices: 26.7 us -> 12.2 us
  starting transfers between devices: 35.9 us -> 25.3 us
  Pallas kernels: 13.1 us -> 11.4 us
  local copies, waits for them, and re-layouts: 2.72 us -> 1.53 us
    all_to_all x1 -> x3, blocking collectives: 13.6 us -> 40.7 us  [exchange(): return lax.all_to_all(array, axis, split_axis=0, concat_axis=0, tiled=True)]
    all_to_all x3 -> x1, waiting for transfers between devices: 22.1 us -> 9.55 us  [exchange(): return lax.all_to_all(array, axis, split_axis=0, concat_axis=0, tiled=True)]
    all_to_all x3 -> x1, starting transfers between devices: 20.3 us -> 8.19 us  [exchange(): return lax.all_to_all(array, axis, split_axis=0, concat_axis=0, tiled=True)]
    ppermute x6, waiting for transfers between devices: 4.63 us -> 2.63 us  [shifted(): return lax.ppermute(array, 'x', [(i, (i + step) % n) for i in range(n)])]
    ppermute x6, starting transfers between devices: 7.91 us -> 9.52 us  [shifted(): return lax.ppermute(array, 'x', [(i, (i + step) % n) for i in range(n)])]
    pallas_call x3, Pallas kernels: 9.54 us -> 8.44 us  [tile_call(): pl.pallas_call(kernel, in_specs=in_vmem(len(tensors)) + [home] + others,...]
  transfers between devices with their start and end apart: 12 -> 10, of which waited for: 5 -> 3; matrix products, arithmetic and copies ran while one was open for 3% -> 2% of each run, Pallas kernels for 6% -> 6%
where the time goes in v4:
time: 93 us; the launch traced here: 92.5 us
  blocking collectives  40.7 us (44%)
  starting transfers between devices  25.3 us (27%)
  waiting for transfers between devices  12.2 us (13%)
  Pallas kernels  11.4 us (12%)
  local copies, waits for them, and re-layouts  1.53 us (2%)
    all_to_all x3, blocking collectives, exchange(): return lax.all_to_all(array, axis, split_axis=0, concat_axis=0, tiled=True)  40.7 us
    all_to_all x1, waiting for transfers between devices, exchange(): return lax.all_to_all(array, axis, split_axis=0, concat_axis=0, tiled=True)  9.55 us
    ppermute x6, starting transfers between devices, shifted(): return lax.ppermute(array, 'x', [(i, (i + step) % n) for i in range(n)])  9.52 us
    pallas_call x3, Pallas kernels, tile_call(): pl.pallas_call(kernel, in_specs=in_vmem(len(tensors)) + [home] + others,...  8.44 us
    all_to_all x1, starting transfers between devices, exchange(): return lax.all_to_all(array, axis, split_axis=0, concat_axis=0, tiled=True)  8.19 us
    ppermute x1, starting transfers between devices, per_device(): opposite = lax.ppermute(codebook, RING_Y, ring)  3.64 us
    ppermute x1, starting transfers between devices, per_device(): across = lax.ppermute(opposite, 'core', swap)  2.75 us
    ppermute x6, waiting for transfers between devices, shifted(): return lax.ppermute(array, 'x', [(i, (i + step) % n) for i in range(n)])  2.63 us
  transfers between devices with their start and end apart: 10, of which 3 were waited for; matrix products, arithmetic and copies ran while one was open for 2% of the time, Pallas kernels for 6%

profile of v4, /device:TPU:1, one launch (start us, length us, event | category | flops | bytes accessed | tf_op | source)
XLA Modules:
  0.0 92.5 jit_solution(138026457477796609)
XLA Ops:
  0.6 3.6 %collective-permute-start = (bf16[1024,384]{1,0:T(8,128)(2,1)}, bf16[1024,384]{1,0:T(8,128)(2,1)S(1)}, u32[]{:S(2)}, u32[]{:S(2)}) collective-permute-start(bf16[1024,384]{1,0:T(8,128)(2,1)} %c0.5), channel_id=1, source_target_pairs={{0,5},{5,0},{1,4},{4,1},{2,7},{7,2},{3,6},{6,3},{8,13},{13,8},{9,1... | collective-permute-start | bytes 2359304 | tf_op jit(solution)/shard_map/ppermute | solution.py:340
  4.3 1.5 %broadcast_in_dim.3 = bf16[8,48,384]{2,1,0:T(8,128)(2,1)} broadcast(bf16[48,384]{1,0:T(8,128)(2,1)} %bitcast.15), dimensions={1,2} | broadcast | bytes 331776 | tf_op jit(solution)/shard_map/broadcast_in_dim | solution.py:27
  5.8 8.2 %all-to-all-start = ((bf16[8,48,384]{2,1,0:T(8,128)(2,1)}), bf16[8,48,384]{2,1,0:T(8,128)(2,1)S(1)}, u32[]{:S(2)}, u32[]{:S(2)}) async-start(bf16[8,48,384]{2,1,0:T(8,128)(2,1)} %broadcast_in_dim.3), calls=%async_computation | async-start | bytes 589824 | tf_op jit(solution)/shard_map/all_to_all | solution.py:22
  14.0 1.2 %collective-permute-start.1 = (bf16[1024,384]{1,0:T(8,128)(2,1)}, bf16[1024,384]{1,0:T(8,128)(2,1)S(1)}, u32[]{:S(2)}, u32[]{:S(2)}) collective-permute-start(bf16[1024,384]{1,0:T(8,128)(2,1)} %c0.5), channel_id=1, source_target_pairs={{0,2},{2,0},{1,3},{3,1},{4,6},{6,4},{5,7},{7,5},{8,10},{10,8},{9,1... | collective-permute-start | bytes 2359304 | tf_op jit(solution)/shard_map/ppermute | solution.py:341
  15.2 9.6 %all-to-all-done = bf16[8,48,384]{2,1,0:T(8,128)(2,1)S(1)} async-done(((bf16[8,48,384]{2,1,0:T(8,128)(2,1)}), bf16[8,48,384]{2,1,0:T(8,128)(2,1)S(1)}, u32[]{:S(2)}, u32[]{:S(2)}) %all-to-all-start) | async-done | bytes 294944 | tf_op jit(solution)/shard_map/all_to_all | solution.py:22
  24.7 0.0 collective-permute-done.c2
  24.7 2.7 %collective-permute-start.2 = (bf16[1024,384]{1,0:T(8,128)(2,1)S(1)}, bf16[1024,384]{1,0:T(8,128)(2,1)S(1)}, u32[]{:S(2)}, u32[]{:S(2)}) collective-permute-start(bf16[1024,384]{1,0:T(8,128)(2,1)S(1)} %collective-permute-done.c2), channel_id=1, source_target_pairs={{0,2},{2,0},{1,3},{3,1},{4,6},{6,4},{5,7},{7,5},{8,10},{10,8},{9,1... | collective-permute-start | bytes 2359304 | tf_op jit(solution)/shard_map/ppermute | solution.py:350
  27.5 2.6 %collective-permute-start.5 = (bf16[192,384]{1,0:T(8,128)(2,1)S(1)}, bf16[192,384]{1,0:T(8,128)(2,1)S(1)}, u32[]{:S(2)}, u32[]{:S(2)}) collective-permute-start(bf16[192,384]{1,0:T(8,128)(2,1)S(1)} %bitcast.13), channel_id=1, source_target_pairs={{0,192},{64,0},{128,64},{192,128},{1,193},{65,1},{129,65},{193,129... | collective-permute-start | bytes 442376 | tf_op jit(solution)/shard_map/ppermute | solution.py:32
  30.1 0.0 collective-permute-start.3
  30.1 2.7 %collective-permute-start.6 = (bf16[192,384]{1,0:T(8,128)(2,1)S(1)}, bf16[192,384]{1,0:T(8,128)(2,1)S(1)}, u32[]{:S(2)}, u32[]{:S(2)}) collective-permute-start(bf16[192,384]{1,0:T(8,128)(2,1)S(1)} %bitcast.11), channel_id=1, source_target_pairs={{0,192},{64,0},{128,64},{192,128},{1,193},{65,1},{129,65},{193,129... | collective-permute-start | bytes 442376 | tf_op jit(solution)/shard_map/ppermute | solution.py:32
  32.8 0.5 collective-permute-done.5.a0
  33.3 0.9 %collective-permute-start.4 = (bf16[192,384]{1,0:T(8,128)(2,1)S(1)}, bf16[192,384]{1,0:T(8,128)(2,1)S(1)}, u32[]{:S(2)}, u32[]{:S(2)}) collective-permute-start(bf16[192,384]{1,0:T(8,128)(2,1)S(1)} %bitcast.12), channel_id=1, source_target_pairs={{0,64},{64,128},{128,192},{192,0},{1,65},{65,129},{129,193},{193,1... | collective-permute-start | bytes 442376 | tf_op jit(solution)/shard_map/ppermute | solution.py:32
  34.2 0.1 turned_of.1.line
  34.3 2.1 %collective-permute-done.3.b0 = bf16[192,384]{1,0:T(8,128)(2,1)S(1)} collective-permute-done((bf16[192,384]{1,0:T(8,128)(2,1)S(1)}, bf16[192,384]{1,0:T(8,128)(2,1)S(1)}, u32[]{:S(2)}, u32[]{:S(2)}) %collective-permute-start.3) | collective-permute-done | bytes 147488 | tf_op jit(solution)/shard_map/ppermute | solution.py:32
  36.4 0.0 collective-permute-start.7
  36.4 0.0 collective-permute-done.6.a1
  36.4 3.4 %collective-permute-start.8 = (bf16[192,384]{1,0:T(8,128)(2,1)S(1)}, bf16[192,384]{1,0:T(8,128)(2,1)S(1)}, u32[]{:S(2)}, u32[]{:S(2)}) collective-permute-start(bf16[192,384]{1,0:T(8,128)(2,1)S(1)} %collective-permute-done.6.a1), channel_id=1, source_target_pairs={{0,192},{64,0},{128,64},{192,128},{1,193},{65,1},{129,65},{193,129... | collective-permute-start | bytes 442376 | tf_op jit(solution)/shard_map/ppermute | solution.py:32
  39.8 0.0 collective-permute-done.4.b1
  39.8 0.0 collective-permute-done.1.c1
  39.8 0.0 collective-permute-done.2.c3
  39.8 3.9 %shard_map.50 = (f32[4096,768]{1,0:T(8,128)S(1)}, f32[32,768]{1,0:T(8,128)S(1)}, f32[32,768]{1,0:T(8,128)S(1)}) custom-call(bf16[192,384]{1,0:T(8,128)(2,1)S(1)} %collective-permute-done.3.b0, bf16[192,384]{1,0:T(8,128)(2,1)S(1)} %collective-permute-done.4.b1, bf16[192,384]{1,0:T(8,128)(2,1)S(1)} %collective-permute-done.5.a0, ...), custom_call_target="tpu_custom_call" | custom-call | flops 2415919104 | bytes 12582912 | tf_op jit(solution)/shard_map/pallas_call | solution.py:191
  43.7 1.7 %shard_map.49 = (f32[4096,256]{1,0:T(8,128)S(1)}, f32[16,256]{1,0:T(8,128)S(1)}, f32[16,256]{1,0:T(8,128)S(1)}) custom-call(bf16[384,256]{1,0:T(8,128)(2,1)S(1)} %turned_of.1.line, bf16[1024,384]{1,0:T(8,128)(2,1)} %c0.5, bf16[1024,384]{1,0:T(8,128)(2,1)S(1)} %collective-permute-done.1.c1, bf16[1024,384]{1,0:T(8,128)(2,1)S(1)} %collective-permute-done.c2, ...), custom_call_target="tpu_custom_call" | custom-call | flops 805306368 | bytes 4194304 | tf_op jit(solution)/shard_map/pallas_call | solution.py:191
  45.4 0.0 collective-permute-done.7.f0
  45.4 0.0 collective-permute-done.8.f1
  45.4 2.9 %shard_map.51 = (f32[4096,512]{1,0:T(8,128)S(1)}, f32[32,512]{1,0:T(8,128)S(1)}, f32[384,128]{1,0:T(8,128)S(1)}) custom-call(bf16[192,384]{1,0:T(8,128)(2,1)S(1)} %collective-permute-done.7.f0, bf16[192,384]{1,0:T(8,128)(2,1)S(1)} %collective-permute-done.8.f1, bf16[384,384]{1,0:T(8,128)(2,1)S(1)} %bitcast.8, bf16[1024,384]{1,0:T(8,128)(2,1)} %c0.5, ...), custom_call_target="tpu_custom_call" | custom-call | flops 1610612736 | bytes 8388608 | tf_op jit(solution)/shard_map/pallas_call | solution.py:191
  48.3 13.9 %all_to_all.20 = f32[32,1,1536]{2,1,0:T(1,128)S(1)} all-to-all(f32[32,1,1536]{2,1,0:T(1,128)S(1)} %bitcast.10), channel_id=1, replica_groups=mesh['x'=4,'z'=8,'yh'=2,'core'=2,'rep'=2] {'x','z'}, dimensions={0} | all-to-all | bytes 393216 | tf_op jit(solution)/shard_map/all_to_all | solution.py:22
  62.2 2.3 %usage_of.1 = (f32[1,48]{1,0:T(1,128)}, f32[8,32,128]{2,1,0:T(8,128)S(1)}) custom-call(f32[4096,256]{1,0:T(8,128)S(1)} %get-tuple-element.20.own_probs, f32[16,256]{1,0:T(8,128)S(1)} %get-tuple-element.21.own_high, f32[4096,768]{1,0:T(8,128)S(1)} %get-tuple-element.22.near_probs, f32[32,768]{1,0:T(8,128)S(1)} %get-tuple-element.23.near_high, ...), custom_call_target="tpu_custom_call" | custom-call | flops 12582912 | bytes 25165824 | tf_op jit(solution)/shard_map/usage_of/pallas_call | solution.py:281
  64.4 14.3 %all_to_all.21.counts = f32[8,32,128]{2,1,0:T(8,128)S(1)} all-to-all(f32[8,32,128]{2,1,0:T(8,128)S(1)} %get-tuple-element.30), channel_id=1, replica_groups=mesh['x'=4,'z'=8,'yh'=2,'core'=2,'rep'=2] {'yh','core','rep'}, dimensions={0} | all-to-all | bytes 262144 | tf_op jit(solution)/shard_map/all_to_all | solution.py:22
  78.8 0.6 entropy_of.1
  79.4 12.5 %all_to_all.22 = f32[32,1,128]{2,1,0:T(1,128)S(1)} all-to-all(f32[32,1,128]{2,1,0:T(1,128)S(1)} %get-tuple-element.32), channel_id=1, replica_groups=mesh['x'=4,'z'=8,'yh'=2,'core'=2,'rep'=2] {'x','z'}, dimensions={0} | all-to-all | bytes 32768 | tf_op jit(solution)/shard_map/all_to_all | solution.py:22
  91.9 0.6 slice_reduce_fusion
  (1 shorter events, 0.0 us)
Async XLA Ops:
  0.6 24.1 %collective-permute-start = (bf16[1024,384]{1,0:T(8,128)(2,1)}, bf16[1024,384]{1,0:T(8,128)(2,1)S(1)}, u32[]{:S(2)}, u32[]{:S(2)}) collective-permute-start(bf16[1024,384]{1,0:T(8,128)(2,1)} %c0.5), channel_id=1, source_target_pairs={{0,5},{5,0},{1,4},{4,1},{2,7},{7,2},{3,6},{6,3},{8,13},{13,8},{9,1... | collective-permute-start | bytes 2359304 | tf_op jit(solution)/shard_map/ppermute | solution.py:340
  5.8 19.0 %all-to-all-start = ((bf16[8,48,384]{2,1,0:T(8,128)(2,1)}), bf16[8,48,384]{2,1,0:T(8,128)(2,1)S(1)}, u32[]{:S(2)}, u32[]{:S(2)}) async-start(bf16[8,48,384]{2,1,0:T(8,128)(2,1)} %broadcast_in_dim.3), calls=%async_computation | async-start | bytes 589824 | tf_op jit(solution)/shard_map/all_to_all | solution.py:22
  14.0 25.8 %collective-permute-start.1 = (bf16[1024,384]{1,0:T(8,128)(2,1)}, bf16[1024,384]{1,0:T(8,128)(2,1)S(1)}, u32[]{:S(2)}, u32[]{:S(2)}) collective-permute-start(bf16[1024,384]{1,0:T(8,128)(2,1)} %c0.5), channel_id=1, source_target_pairs={{0,2},{2,0},{1,3},{3,1},{4,6},{6,4},{5,7},{7,5},{8,10},{10,8},{9,1... | collective-permute-start | bytes 2359304 | tf_op jit(solution)/shard_map/ppermute | solution.py:341
  24.7 15.0 %collective-permute-start.2 = (bf16[1024,384]{1,0:T(8,128)(2,1)S(1)}, bf16[1024,384]{1,0:T(8,128)(2,1)S(1)}, u32[]{:S(2)}, u32[]{:S(2)}) collective-permute-start(bf16[1024,384]{1,0:T(8,128)(2,1)S(1)} %collective-permute-done.c2), channel_id=1, source_target_pairs={{0,2},{2,0},{1,3},{3,1},{4,6},{6,4},{5,7},{7,5},{8,10},{10,8},{9,1... | collective-permute-start | bytes 2359304 | tf_op jit(solution)/shard_map/ppermute | solution.py:350
  27.5 5.8 %collective-permute-start.5 = (bf16[192,384]{1,0:T(8,128)(2,1)S(1)}, bf16[192,384]{1,0:T(8,128)(2,1)S(1)}, u32[]{:S(2)}, u32[]{:S(2)}) collective-permute-start(bf16[192,384]{1,0:T(8,128)(2,1)S(1)} %bitcast.13), channel_id=1, source_target_pairs={{0,192},{64,0},{128,64},{192,128},{1,193},{65,1},{129,65},{193,129... | collective-permute-start | bytes 442376 | tf_op jit(solution)/shard_map/ppermute | solution.py:32
  30.1 6.3 %collective-permute-start.3 = (bf16[192,384]{1,0:T(8,128)(2,1)S(1)}, bf16[192,384]{1,0:T(8,128)(2,1)S(1)}, u32[]{:S(2)}, u32[]{:S(2)}) collective-permute-start(bf16[192,384]{1,0:T(8,128)(2,1)S(1)} %bitcast.14), channel_id=1, source_target_pairs={{0,64},{64,128},{128,192},{192,0},{1,65},{65,129},{129,193},{193,1... | collective-permute-start | bytes 442376 | tf_op jit(solution)/shard_map/ppermute | solution.py:32
  30.1 6.3 %collective-permute-start.6 = (bf16[192,384]{1,0:T(8,128)(2,1)S(1)}, bf16[192,384]{1,0:T(8,128)(2,1)S(1)}, u32[]{:S(2)}, u32[]{:S(2)}) collective-permute-start(bf16[192,384]{1,0:T(8,128)(2,1)S(1)} %bitcast.11), channel_id=1, source_target_pairs={{0,192},{64,0},{128,64},{192,128},{1,193},{65,1},{129,65},{193,129... | collective-permute-start | bytes 442376 | tf_op jit(solution)/shard_map/ppermute | solution.py:32
  33.3 6.5 %collective-permute-start.4 = (bf16[192,384]{1,0:T(8,128)(2,1)S(1)}, bf16[192,384]{1,0:T(8,128)(2,1)S(1)}, u32[]{:S(2)}, u32[]{:S(2)}) collective-permute-start(bf16[192,384]{1,0:T(8,128)(2,1)S(1)} %bitcast.12), channel_id=1, source_target_pairs={{0,64},{64,128},{128,192},{192,0},{1,65},{65,129},{129,193},{193,1... | collective-permute-start | bytes 442376 | tf_op jit(solution)/shard_map/ppermute | solution.py:32
  36.4 9.0 %collective-permute-start.7 = (bf16[192,384]{1,0:T(8,128)(2,1)S(1)}, bf16[192,384]{1,0:T(8,128)(2,1)S(1)}, u32[]{:S(2)}, u32[]{:S(2)}) collective-permute-start(bf16[192,384]{1,0:T(8,128)(2,1)S(1)} %collective-permute-done.3.b0), channel_id=1, source_target_pairs={{0,64},{64,128},{128,192},{192,0},{1,65},{65,129},{129,193},{193,1... | collective-permute-start | bytes 442376 | tf_op jit(solution)/shard_map/ppermute | solution.py:32
  36.4 9.0 %collective-permute-start.8 = (bf16[192,384]{1,0:T(8,128)(2,1)S(1)}, bf16[192,384]{1,0:T(8,128)(2,1)S(1)}, u32[]{:S(2)}, u32[]{:S(2)}) collective-permute-start(bf16[192,384]{1,0:T(8,128)(2,1)S(1)} %collective-permute-done.6.a1), channel_id=1, source_target_pairs={{0,192},{64,0},{128,64},{192,128},{1,193},{65,1},{129,65},{193,129... | collective-permute-start | bytes 442376 | tf_op jit(solution)/shard_map/ppermute | solution.py:32

commit v5 on v4

--- a/solution.py
+++ b/solution.py
@@ -82,13 +82,13 @@
     )
 
 
-def turned_kernel(line, out):
-    out[...] = line[pl.ds(0, out.shape[1]), :].T
-
-
-def turned_of(line, count):
+def turned_kernel(start, line, out):
+    out[...] = line[pl.ds(start, out.shape[1]), :].T
+
+
+def turned_of(line, start, count):
     return pl.pallas_call(
-        turned_kernel,
+        functools.partial(turned_kernel, start),
         in_specs=in_vmem(1),
         out_specs=in_vmem(1)[0],
         out_shape=jax.ShapeDtypeStruct((line.shape[1], count), line.dtype),
@@ -127,13 +127,13 @@
 
 
 def far_kernel(
-    f0, f1, line, c0, c1, c2, c3, own_high, own_total, near_high, near_total,
+    f0, f1, left, c0, c1, c2, c3, own_high, own_total, near_high, near_total,
     probs, high, lse_out, dense, total, turned, sa, sb, home, arrival, joined,
 ):
-    count = line.shape[0]
+    count = joined.shape[0]
     join((f0, f1), joined)
     turned[:, pl.ds(0, count)] = joined[...].T
-    turned[:, pl.ds(count, count - HELD)] = line[pl.ds(HELD, count - HELD), :].T
+    turned[:, pl.ds(count, count - HELD)] = left[...]
     codes = (c0, c1, c2, c3)
     tile(codes, turned, probs, high, total, (sa, sb), home, arrival)
 
@@ -346,13 +346,13 @@
     a1 = shifted(line[half:], -1)
     b1 = shifted(line[half:], 1)
     a0 = shifted(line[:half], -1)
-    opposite, line = lax.optimization_barrier((opposite, line))
     across = lax.ppermute(opposite, "core", swap)
     f0 = shifted(b0, 1)
     f1 = shifted(a1, -1)
     home = pltpu.with_memory_space_constraint(codebook, pltpu.HBM)
     codes = (home, beside, opposite, across)
-    turned = turned_of(line, HELD)
+    turned = turned_of(line, 0, HELD)
+    left = turned_of(line, HELD, count - HELD)
     own_probs, own_high, own_total = tile_call(
         own_kernel, (turned,), codes, (), HELD, 256
     )
@@ -361,7 +361,7 @@
     )
     stats = (own_high, own_total, near_high, near_total)
     far_probs, far_high, part = tile_call(
-        far_kernel, (f0, f1, line), codes, stats, 2 * count - HELD, 128,
+        far_kernel, (f0, f1, left), codes, stats, 2 * count - HELD, 128,
         (plane * 4 * count // LANES, LANES),
     )
     parts = exchange(part.reshape(plane, 1, 4 * count), PLANE).reshape(part.shape)

time: 93 us -> 93 us (level)
  blocking collectives: 40.7 us -> 43.9 us
  waiting for transfers between devices: 12.2 us -> 10.3 us
  starting transfers between devices: 25.3 us -> 23.9 us
    all_to_all x1, waiting for transfers between devices: 9.55 us -> 1.76 us  [exchange(): return lax.all_to_all(array, axis, split_axis=0, concat_axis=0, tiled=True)]
    ppermute x1, waiting for transfers between devices: 0.01 us -> 5.62 us  [per_device(): opposite = lax.ppermute(codebook, RING_Y, ring)]
    all_to_all x3, blocking collectives: 40.7 us -> 43.9 us  [exchange(): return lax.all_to_all(array, axis, split_axis=0, concat_axis=0, tiled=True)]
  transfers between devices with their start and end apart: 10 -> 10, of which waited for: 3 -> 4; matrix products, arithmetic and copies ran while one was open for 2% -> 2% of each run, Pallas kernels for 6% -> 6%
where the time goes in v5:
time: 93 us; the launch traced here: 92.6 us
  blocking collectives  43.9 us (47%)
  starting transfers between devices  23.9 us (26%)
  Pallas kernels  11.6 us (12%)
  waiting for transfers between devices  10.3 us (11%)
  local copies, waits for them, and re-layouts  1.53 us (2%)
    all_to_all x3, blocking collectives, exchange(): return lax.all_to_all(array, axis, split_axis=0, concat_axis=0, tiled=True)  43.9 us
    ppermute x6, starting transfers between devices, shifted(): return lax.ppermute(array, 'x', [(i, (i + step) % n) for i in range(n)])  8.69 us
    pallas_call x3, Pallas kernels, tile_call(): pl.pallas_call(kernel, in_specs=in_vmem(len(tensors)) + [home] + others,...  8.51 us
    all_to_all x1, starting transfers between devices, exchange(): return lax.all_to_all(array, axis, split_axis=0, concat_axis=0, tiled=True)  8.19 us
    ppermute x1, waiting for transfers between devices, per_device(): opposite = lax.ppermute(codebook, RING_Y, ring)  5.62 us
    ppermute x1, starting transfers between devices, per_device(): opposite = lax.ppermute(codebook, RING_Y, ring)  3.64 us
    ppermute x6, waiting for transfers between devices, shifted(): return lax.ppermute(array, 'x', [(i, (i + step) % n) for i in range(n)])  2.9 us
    pallas_call x1, Pallas kernels, usage_of(): pl.pallas_call(usage_kernel, in_specs=in_vmem(len(held) + 1), out_specs=i...  2.28 us
  transfers between devices with their start and end apart: 10, of which 4 were waited for; matrix products, arithmetic and copies ran while one was open for 2% of the time, Pallas kernels for 6%

profile of v5, /device:TPU:1, one launch (start us, length us, event | category | flops | bytes accessed | tf_op | source)
XLA Modules:
  0.0 92.6 jit_solution(7877228127436172048)
XLA Ops:
  0.6 3.6 %collective-permute-start.1 = (bf16[1024,384]{1,0:T(8,128)(2,1)}, bf16[1024,384]{1,0:T(8,128)(2,1)S(1)}, u32[]{:S(2)}, u32[]{:S(2)}) collective-permute-start(bf16[1024,384]{1,0:T(8,128)(2,1)} %c0.5), channel_id=1, source_target_pairs={{0,5},{5,0},{1,4},{4,1},{2,7},{7,2},{3,6},{6,3},{8,13},{13,8},{9,1... | collective-permute-start | bytes 2359304 | tf_op jit(solution)/shard_map/ppermute | solution.py:340
  4.3 1.5 %broadcast_in_dim.3 = bf16[8,48,384]{2,1,0:T(8,128)(2,1)} broadcast(bf16[48,384]{1,0:T(8,128)(2,1)} %bitcast.15), dimensions={1,2} | broadcast | bytes 331776 | tf_op jit(solution)/shard_map/broadcast_in_dim | solution.py:27
  5.8 8.2 %all-to-all-start = ((bf16[8,48,384]{2,1,0:T(8,128)(2,1)}), bf16[8,48,384]{2,1,0:T(8,128)(2,1)S(1)}, u32[]{:S(2)}, u32[]{:S(2)}) async-start(bf16[8,48,384]{2,1,0:T(8,128)(2,1)} %broadcast_in_dim.3), calls=%async_computation | async-start | bytes 589824 | tf_op jit(solution)/shard_map/all_to_all | solution.py:22
  14.0 1.2 %collective-permute-start = (bf16[1024,384]{1,0:T(8,128)(2,1)}, bf16[1024,384]{1,0:T(8,128)(2,1)S(1)}, u32[]{:S(2)}, u32[]{:S(2)}) collective-permute-start(bf16[1024,384]{1,0:T(8,128)(2,1)} %c0.5), channel_id=1, source_target_pairs={{0,2},{2,0},{1,3},{3,1},{4,6},{6,4},{5,7},{7,5},{8,10},{10,8},{9,1... | collective-permute-start | bytes 2359304 | tf_op jit(solution)/shard_map/ppermute | solution.py:341
  15.2 5.6 %collective-permute-done.1.c2 = bf16[1024,384]{1,0:T(8,128)(2,1)S(1)} collective-permute-done((bf16[1024,384]{1,0:T(8,128)(2,1)}, bf16[1024,384]{1,0:T(8,128)(2,1)S(1)}, u32[]{:S(2)}, u32[]{:S(2)}) %collective-permute-start.1) | collective-permute-done | bytes 786464 | tf_op jit(solution)/shard_map/ppermute | solution.py:340
  20.8 2.2 %collective-permute-start.2 = (bf16[1024,384]{1,0:T(8,128)(2,1)S(1)}, bf16[1024,384]{1,0:T(8,128)(2,1)S(1)}, u32[]{:S(2)}, u32[]{:S(2)}) collective-permute-start(bf16[1024,384]{1,0:T(8,128)(2,1)S(1)} %collective-permute-done.1.c2), channel_id=1, source_target_pairs={{0,2},{2,0},{1,3},{3,1},{4,6},{6,4},{5,7},{7,5},{8,10},{10,8},{9,1... | collective-permute-start | bytes 2359304 | tf_op jit(solution)/shard_map/ppermute | solution.py:349
  23.0 1.8 %all-to-all-done = bf16[8,48,384]{2,1,0:T(8,128)(2,1)S(1)} async-done(((bf16[8,48,384]{2,1,0:T(8,128)(2,1)}), bf16[8,48,384]{2,1,0:T(8,128)(2,1)S(1)}, u32[]{:S(2)}, u32[]{:S(2)}) %all-to-all-start) | async-done | bytes 294944 | tf_op jit(solution)/shard_map/all_to_all | solution.py:22
  24.8 2.6 %collective-permute-start.5 = (bf16[192,384]{1,0:T(8,128)(2,1)S(1)}, bf16[192,384]{1,0:T(8,128)(2,1)S(1)}, u32[]{:S(2)}, u32[]{:S(2)}) collective-permute-start(bf16[192,384]{1,0:T(8,128)(2,1)S(1)} %bitcast.13), channel_id=1, source_target_pairs={{0,192},{64,0},{128,64},{192,128},{1,193},{65,1},{129,65},{193,129... | collective-permute-start | bytes 442376 | tf_op jit(solution)/shard_map/ppermute | solution.py:32
  27.3 0.0 collective-permute-start.3
  27.3 2.7 %collective-permute-start.6 = (bf16[192,384]{1,0:T(8,128)(2,1)S(1)}, bf16[192,384]{1,0:T(8,128)(2,1)S(1)}, u32[]{:S(2)}, u32[]{:S(2)}) collective-permute-start(bf16[192,384]{1,0:T(8,128)(2,1)S(1)} %bitcast.11), channel_id=1, source_target_pairs={{0,192},{64,0},{128,64},{192,128},{1,193},{65,1},{129,65},{193,129... | collective-permute-start | bytes 442376 | tf_op jit(solution)/shard_map/ppermute | solution.py:32
  30.0 0.0 collective-permute-done.5.a0
  30.0 0.0 collective-permute-start.4
  30.1 0.1 turned_of.3.left
  30.1 0.1 turned_of.2.line
  30.3 2.3 %collective-permute-done.3.b0 = bf16[192,384]{1,0:T(8,128)(2,1)S(1)} collective-permute-done((bf16[192,384]{1,0:T(8,128)(2,1)S(1)}, bf16[192,384]{1,0:T(8,128)(2,1)S(1)}, u32[]{:S(2)}, u32[]{:S(2)}) %collective-permute-start.3) | collective-permute-done | bytes 147488 | tf_op jit(solution)/shard_map/ppermute | solution.py:32
  32.5 0.0 collective-permute-start.7
  32.5 0.6 collective-permute-done.6.a1
  33.1 3.4 %collective-permute-start.8 = (bf16[192,384]{1,0:T(8,128)(2,1)S(1)}, bf16[192,384]{1,0:T(8,128)(2,1)S(1)}, u32[]{:S(2)}, u32[]{:S(2)}) collective-permute-start(bf16[192,384]{1,0:T(8,128)(2,1)S(1)} %collective-permute-done.6.a1), channel_id=1, source_target_pairs={{0,192},{64,0},{128,64},{192,128},{1,193},{65,1},{129,65},{193,129... | collective-permute-start | bytes 442376 | tf_op jit(solution)/shard_map/ppermute | solution.py:32
  36.6 0.0 collective-permute-done.4.b1
  36.6 0.0 collective-permute-done.c1
  36.6 0.0 collective-permute-done.2.c3
  36.6 3.9 %shard_map.50 = (f32[4096,768]{1,0:T(8,128)S(1)}, f32[32,768]{1,0:T(8,128)S(1)}, f32[32,768]{1,0:T(8,128)S(1)}) custom-call(bf16[192,384]{1,0:T(8,128)(2,1)S(1)} %collective-permute-done.3.b0, bf16[192,384]{1,0:T(8,128)(2,1)S(1)} %collective-permute-done.4.b1, bf16[192,384]{1,0:T(8,128)(2,1)S(1)} %collective-permute-done.5.a0, ...), custom_call_target="tpu_custom_call" | custom-call | flops 2415919104 | bytes 12582912 | tf_op jit(solution)/shard_map/pallas_call | solution.py:191
  40.5 1.7 %shard_map.49 = (f32[4096,256]{1,0:T(8,128)S(1)}, f32[16,256]{1,0:T(8,128)S(1)}, f32[16,256]{1,0:T(8,128)S(1)}) custom-call(bf16[384,256]{1,0:T(8,128)(2,1)S(1)} %turned_of.2.line, bf16[1024,384]{1,0:T(8,128)(2,1)} %c0.5, bf16[1024,384]{1,0:T(8,128)(2,1)S(1)} %collective-permute-done.c1, bf16[1024,384]{1,0:T(8,128)(2,1)S(1)} %collective-permute-done.1.c2, ...), custom_call_target="tpu_custom_call" | custom-call | flops 805306368 | bytes 4194304 | tf_op jit(solution)/shard_map/pallas_call | solution.py:191
  42.2 0.0 collective-permute-done.7.f0
  42.2 0.0 collective-permute-done.8.f1
  42.2 2.9 %shard_map.51 = (f32[4096,512]{1,0:T(8,128)S(1)}, f32[32,512]{1,0:T(8,128)S(1)}, f32[384,128]{1,0:T(8,128)S(1)}) custom-call(bf16[192,384]{1,0:T(8,128)(2,1)S(1)} %collective-permute-done.7.f0, bf16[192,384]{1,0:T(8,128)(2,1)S(1)} %collective-permute-done.8.f1, bf16[384,128]{1,0:T(8,128)(2,1)S(1)} %turned_of.3.left, bf16[1024,384]{1,0:T(8,128)(2,1)} %c0.5, ...), custom_call_target="tpu_custom_call" | custom-call | flops 1610612736 | bytes 8388608 | tf_op jit(solution)/shard_map/pallas_call | solution.py:191
  45.1 17.1 %all_to_all.20 = f32[32,1,1536]{2,1,0:T(1,128)S(1)} all-to-all(f32[32,1,1536]{2,1,0:T(1,128)S(1)} %bitcast.10), channel_id=1, replica_groups=mesh['x'=4,'z'=8,'yh'=2,'core'=2,'rep'=2] {'x','z'}, dimensions={0} | all-to-all | bytes 393216 | tf_op jit(solution)/shard_map/all_to_all | solution.py:22
  62.2 2.3 %usage_of.1 = (f32[1,48]{1,0:T(1,128)}, f32[8,32,128]{2,1,0:T(8,128)S(1)}) custom-call(f32[4096,256]{1,0:T(8,128)S(1)} %get-tuple-element.16.own_probs, f32[16,256]{1,0:T(8,128)S(1)} %get-tuple-element.17.own_high, f32[4096,768]{1,0:T(8,128)S(1)} %get-tuple-element.18.near_probs, f32[32,768]{1,0:T(8,128)S(1)} %get-tuple-element.19.near_high, ...), custom_call_target="tpu_custom_call" | custom-call | flops 12582912 | bytes 25165824 | tf_op jit(solution)/shard_map/usage_of/pallas_call | solution.py:281
  64.5 14.3 %all_to_all.21.counts = f32[8,32,128]{2,1,0:T(8,128)S(1)} all-to-all(f32[8,32,128]{2,1,0:T(8,128)S(1)} %get-tuple-element.26), channel_id=1, replica_groups=mesh['x'=4,'z'=8,'yh'=2,'core'=2,'rep'=2] {'yh','core','rep'}, dimensions={0} | all-to-all | bytes 262144 | tf_op jit(solution)/shard_map/all_to_all | solution.py:22
  78.8 0.6 entropy_of.1
  79.5 12.5 %all_to_all.22 = f32[32,1,128]{2,1,0:T(1,128)S(1)} all-to-all(f32[32,1,128]{2,1,0:T(1,128)S(1)} %get-tuple-element.28), channel_id=1, replica_groups=mesh['x'=4,'z'=8,'yh'=2,'core'=2,'rep'=2] {'x','z'}, dimensions={0} | all-to-all | bytes 32768 | tf_op jit(solution)/shard_map/all_to_all | solution.py:22
  91.9 0.6 slice_reduce_fusion
  (1 shorter events, 0.0 us)
Async XLA Ops:
  0.6 20.2 %collective-permute-start.1 = (bf16[1024,384]{1,0:T(8,128)(2,1)}, bf16[1024,384]{1,0:T(8,128)(2,1)S(1)}, u32[]{:S(2)}, u32[]{:S(2)}) collective-permute-start(bf16[1024,384]{1,0:T(8,128)(2,1)} %c0.5), channel_id=1, source_target_pairs={{0,5},{5,0},{1,4},{4,1},{2,7},{7,2},{3,6},{6,3},{8,13},{13,8},{9,1... | collective-permute-start | bytes 2359304 | tf_op jit(solution)/shard_map/ppermute | solution.py:340
  5.8 19.0 %all-to-all-start = ((bf16[8,48,384]{2,1,0:T(8,128)(2,1)}), bf16[8,48,384]{2,1,0:T(8,128)(2,1)S(1)}, u32[]{:S(2)}, u32[]{:S(2)}) async-start(bf16[8,48,384]{2,1,0:T(8,128)(2,1)} %broadcast_in_dim.3), calls=%async_computation | async-start | bytes 589824 | tf_op jit(solution)/shard_map/all_to_all | solution.py:22
  14.0 22.6 %collective-permute-start = (bf16[1024,384]{1,0:T(8,128)(2,1)}, bf16[1024,384]{1,0:T(8,128)(2,1)S(1)}, u32[]{:S(2)}, u32[]{:S(2)}) collective-permute-start(bf16[1024,384]{1,0:T(8,128)(2,1)} %c0.5), channel_id=1, source_target_pairs={{0,2},{2,0},{1,3},{3,1},{4,6},{6,4},{5,7},{7,5},{8,10},{10,8},{9,1... | collective-permute-start | bytes 2359304 | tf_op jit(solution)/shard_map/ppermute | solution.py:341
  20.8 15.8 %collective-permute-start.2 = (bf16[1024,384]{1,0:T(8,128)(2,1)S(1)}, bf16[1024,384]{1,0:T(8,128)(2,1)S(1)}, u32[]{:S(2)}, u32[]{:S(2)}) collective-permute-start(bf16[1024,384]{1,0:T(8,128)(2,1)S(1)} %collective-permute-done.1.c2), channel_id=1, source_target_pairs={{0,2},{2,0},{1,3},{3,1},{4,6},{6,4},{5,7},{7,5},{8,10},{10,8},{9,1... | collective-permute-start | bytes 2359304 | tf_op jit(solution)/shard_map/ppermute | solution.py:349
  24.8 5.2 %collective-permute-start.5 = (bf16[192,384]{1,0:T(8,128)(2,1)S(1)}, bf16[192,384]{1,0:T(8,128)(2,1)S(1)}, u32[]{:S(2)}, u32[]{:S(2)}) collective-permute-start(bf16[192,384]{1,0:T(8,128)(2,1)S(1)} %bitcast.13), channel_id=1, source_target_pairs={{0,192},{64,0},{128,64},{192,128},{1,193},{65,1},{129,65},{193,129... | collective-permute-start | bytes 442376 | tf_op jit(solution)/shard_map/ppermute | solution.py:32
  27.3 5.2 %collective-permute-start.3 = (bf16[192,384]{1,0:T(8,128)(2,1)S(1)}, bf16[192,384]{1,0:T(8,128)(2,1)S(1)}, u32[]{:S(2)}, u32[]{:S(2)}) collective-permute-start(bf16[192,384]{1,0:T(8,128)(2,1)S(1)} %bitcast.14), channel_id=1, source_target_pairs={{0,64},{64,128},{128,192},{192,0},{1,65},{65,129},{129,193},{193,1... | collective-permute-start | bytes 442376 | tf_op jit(solution)/shard_map/ppermute | solution.py:32
  27.3 5.8 %collective-permute-start.6 = (bf16[192,384]{1,0:T(8,128)(2,1)S(1)}, bf16[192,384]{1,0:T(8,128)(2,1)S(1)}, u32[]{:S(2)}, u32[]{:S(2)}) collective-permute-start(bf16[192,384]{1,0:T(8,128)(2,1)S(1)} %bitcast.11), channel_id=1, source_target_pairs={{0,192},{64,0},{128,64},{192,128},{1,193},{65,1},{129,65},{193,129... | collective-permute-start | bytes 442376 | tf_op jit(solution)/shard_map/ppermute | solution.py:32
  30.0 6.5 %collective-permute-start.4 = (bf16[192,384]{1,0:T(8,128)(2,1)S(1)}, bf16[192,384]{1,0:T(8,128)(2,1)S(1)}, u32[]{:S(2)}, u32[]{:S(2)}) collective-permute-start(bf16[192,384]{1,0:T(8,128)(2,1)S(1)} %bitcast.12), channel_id=1, source_target_pairs={{0,64},{64,128},{128,192},{192,0},{1,65},{65,129},{129,193},{193,1... | collective-permute-start | bytes 442376 | tf_op jit(solution)/shard_map/ppermute | solution.py:32
  32.5 9.6 %collective-permute-start.7 = (bf16[192,384]{1,0:T(8,128)(2,1)S(1)}, bf16[192,384]{1,0:T(8,128)(2,1)S(1)}, u32[]{:S(2)}, u32[]{:S(2)}) collective-permute-start(bf16[192,384]{1,0:T(8,128)(2,1)S(1)} %collective-permute-done.3.b0), channel_id=1, source_target_pairs={{0,64},{64,128},{128,192},{192,0},{1,65},{65,129},{129,193},{193,1... | collective-permute-start | bytes 442376 | tf_op jit(solution)/shard_map/ppermute | solution.py:32
  33.1 9.0 %collective-permute-start.8 = (bf16[192,384]{1,0:T(8,128)(2,1)S(1)}, bf16[192,384]{1,0:T(8,128)(2,1)S(1)}, u32[]{:S(2)}, u32[]{:S(2)}) collective-permute-start(bf16[192,384]{1,0:T(8,128)(2,1)S(1)} %collective-permute-done.6.a1), channel_id=1, source_target_pairs={{0,192},{64,0},{128,64},{192,128},{1,193},{65,1},{129,65},{193,129... | collective-permute-start | bytes 442376 | tf_op jit(solution)/shard_map/ppermute | solution.py:32

commit v6 on v4

--- a/solution.py
+++ b/solution.py
@@ -205,7 +205,7 @@
 
 def usage_kernel(
     own_probs, own_high, near_probs, near_high, far_probs, far_high, parts,
-    own_out, usage_out, lse_out, column,
+    own_out, usage_out, lse_out, column, shown_lse, leaving,
 ):
     count = near_probs.shape[1] // 2
     left = count - HELD
@@ -228,7 +228,7 @@
         mass = mass + jnp.exp(parts[pl.ds(k, 2 * lines), :] - twice)
     lse_out[...] = peak + jnp.log(both(jnp.add, mass))
 
-    shown = own_out.shape[1]
+    shown = shown_lse.shape[1]
     at = lax.axis_index(PLANE) * shown
     row, shift = at // LANES, lax.rem(LANES - lax.rem(at, LANES), LANES)
     first = pltpu.roll(lse_out[pl.ds(row, 1), :], shift, 1)
@@ -236,7 +236,9 @@
     second = pltpu.roll(second, shift, 1)
     lane = lax.broadcasted_iota(jnp.int32, (1, LANES), 1)
     straddle = jnp.logical_and(shift > 0, lane >= shift)
-    own_out[...] = jnp.where(straddle, second, first)[:, :shown]
+    shown_lse[...] = jnp.where(straddle, second, first)[:, :shown]
+    leave = pltpu.make_async_copy(shown_lse, own_out, leaving)
+    leave.start()
 
     yh, core = lax.axis_index("yh"), lax.axis_index("core")
     held = []
@@ -272,6 +274,7 @@
         column[pl.ds(owner * each + g % each, 1), :] = line
     for k in range(usage_out.shape[0]):
         usage_out[k] = column[...]
+    leave.wait()
 
 
 def usage_of(held, parts, copies, shown):
@@ -281,7 +284,7 @@
     return pl.pallas_call(
         usage_kernel,
         in_specs=in_vmem(len(held) + 1),
-        out_specs=in_vmem(2),
+        out_specs=[pl.BlockSpec(memory_space=pltpu.HBM)] + in_vmem(1),
         out_shape=[
             jax.ShapeDtypeStruct((1, shown), f32),
             jax.ShapeDtypeStruct((copies, protos // LANES, LANES), f32),
@@ -289,6 +292,8 @@
         scratch_shapes=[
             pltpu.VMEM((total // LANES, LANES), f32),
             pltpu.VMEM((protos // LANES, LANES), f32),
+            pltpu.VMEM((1, shown), f32),
+            pltpu.SemaphoreType.DMA,
         ],
         compiler_params=pltpu.CompilerParams(vmem_limit_bytes=8 * 1024 * 1024),
         cost_estimate=pl.CostEstimate(

time: 93 us -> 93 us (level)
  no operation moved by 1% of the time
where the time goes in v6:
time: 93 us; the launch traced here: 92.5 us
  blocking collectives  40.7 us (44%)
  starting transfers between devices  25.3 us (27%)
  waiting for transfers between devices  12.2 us (13%)
  Pallas kernels  11.4 us (12%)
  local copies, waits for them, and re-layouts  1.53 us (2%)
    all_to_all x3, blocking collectives, exchange(): return lax.all_to_all(array, axis, split_axis=0, concat_axis=0, tiled=True)  40.7 us
    all_to_all x1, waiting for transfers between devices, exchange(): return lax.all_to_all(array, axis, split_axis=0, concat_axis=0, tiled=True)  9.55 us
    ppermute x6, starting transfers between devices, shifted(): return lax.ppermute(array, 'x', [(i, (i + step) % n) for i in range(n)])  9.52 us
    pallas_call x3, Pallas kernels, tile_call(): pl.pallas_call(kernel, in_specs=in_vmem(len(tensors)) + [home] + others,...  8.44 us
    all_to_all x1, starting transfers between devices, exchange(): return lax.all_to_all(array, axis, split_axis=0, concat_axis=0, tiled=True)  8.19 us
    ppermute x1, starting transfers between devices, per_device(): opposite = lax.ppermute(codebook, RING_Y, ring)  3.64 us
    ppermute x1, starting transfers between devices, per_device(): across = lax.ppermute(opposite, 'core', swap)  2.75 us
    ppermute x6, waiting for transfers between devices, shifted(): return lax.ppermute(array, 'x', [(i, (i + step) % n) for i in range(n)])  2.63 us
  transfers between devices with their start and end apart: 10, of which 3 were waited for; matrix products, arithmetic and copies ran while one was open for 2% of the time, Pallas kernels for 6%

profile of v6, /device:TPU:1, one launch (start us, length us, event | category | flops | bytes accessed | tf_op | source)
XLA Modules:
  0.0 92.5 jit_solution(14369618781284511846)
XLA Ops:
  0.6 3.6 %collective-permute-start = (bf16[1024,384]{1,0:T(8,128)(2,1)}, bf16[1024,384]{1,0:T(8,128)(2,1)S(1)}, u32[]{:S(2)}, u32[]{:S(2)}) collective-permute-start(bf16[1024,384]{1,0:T(8,128)(2,1)} %c0.5), channel_id=1, source_target_pairs={{0,5},{5,0},{1,4},{4,1},{2,7},{7,2},{3,6},{6,3},{8,13},{13,8},{9,1... | collective-permute-start | bytes 2359304 | tf_op jit(solution)/shard_map/ppermute | solution.py:345
  4.3 1.5 %broadcast_in_dim.3 = bf16[8,48,384]{2,1,0:T(8,128)(2,1)} broadcast(bf16[48,384]{1,0:T(8,128)(2,1)} %bitcast.15), dimensions={1,2} | broadcast | bytes 331776 | tf_op jit(solution)/shard_map/broadcast_in_dim | solution.py:27
  5.8 8.2 %all-to-all-start = ((bf16[8,48,384]{2,1,0:T(8,128)(2,1)}), bf16[8,48,384]{2,1,0:T(8,128)(2,1)S(1)}, u32[]{:S(2)}, u32[]{:S(2)}) async-start(bf16[8,48,384]{2,1,0:T(8,128)(2,1)} %broadcast_in_dim.3), calls=%async_computation | async-start | bytes 589824 | tf_op jit(solution)/shard_map/all_to_all | solution.py:22
  14.0 1.2 %collective-permute-start.1 = (bf16[1024,384]{1,0:T(8,128)(2,1)}, bf16[1024,384]{1,0:T(8,128)(2,1)S(1)}, u32[]{:S(2)}, u32[]{:S(2)}) collective-permute-start(bf16[1024,384]{1,0:T(8,128)(2,1)} %c0.5), channel_id=1, source_target_pairs={{0,2},{2,0},{1,3},{3,1},{4,6},{6,4},{5,7},{7,5},{8,10},{10,8},{9,1... | collective-permute-start | bytes 2359304 | tf_op jit(solution)/shard_map/ppermute | solution.py:346
  15.2 9.6 %all-to-all-done = bf16[8,48,384]{2,1,0:T(8,128)(2,1)S(1)} async-done(((bf16[8,48,384]{2,1,0:T(8,128)(2,1)}), bf16[8,48,384]{2,1,0:T(8,128)(2,1)S(1)}, u32[]{:S(2)}, u32[]{:S(2)}) %all-to-all-start) | async-done | bytes 294944 | tf_op jit(solution)/shard_map/all_to_all | solution.py:22
  24.7 0.0 collective-permute-done.c2
  24.7 2.7 %collective-permute-start.2 = (bf16[1024,384]{1,0:T(8,128)(2,1)S(1)}, bf16[1024,384]{1,0:T(8,128)(2,1)S(1)}, u32[]{:S(2)}, u32[]{:S(2)}) collective-permute-start(bf16[1024,384]{1,0:T(8,128)(2,1)S(1)} %collective-permute-done.c2), channel_id=1, source_target_pairs={{0,2},{2,0},{1,3},{3,1},{4,6},{6,4},{5,7},{7,5},{8,10},{10,8},{9,1... | collective-permute-start | bytes 2359304 | tf_op jit(solution)/shard_map/ppermute | solution.py:355
  27.5 2.6 %collective-permute-start.5 = (bf16[192,384]{1,0:T(8,128)(2,1)S(1)}, bf16[192,384]{1,0:T(8,128)(2,1)S(1)}, u32[]{:S(2)}, u32[]{:S(2)}) collective-permute-start(bf16[192,384]{1,0:T(8,128)(2,1)S(1)} %bitcast.13), channel_id=1, source_target_pairs={{0,192},{64,0},{128,64},{192,128},{1,193},{65,1},{129,65},{193,129... | collective-permute-start | bytes 442376 | tf_op jit(solution)/shard_map/ppermute | solution.py:32
  30.1 0.0 collective-permute-start.3
  30.1 2.7 %collective-permute-start.6 = (bf16[192,384]{1,0:T(8,128)(2,1)S(1)}, bf16[192,384]{1,0:T(8,128)(2,1)S(1)}, u32[]{:S(2)}, u32[]{:S(2)}) collective-permute-start(bf16[192,384]{1,0:T(8,128)(2,1)S(1)} %bitcast.11), channel_id=1, source_target_pairs={{0,192},{64,0},{128,64},{192,128},{1,193},{65,1},{129,65},{193,129... | collective-permute-start | bytes 442376 | tf_op jit(solution)/shard_map/ppermute | solution.py:32
  32.8 0.5 collective-permute-done.5.a0
  33.3 0.9 %collective-permute-start.4 = (bf16[192,384]{1,0:T(8,128)(2,1)S(1)}, bf16[192,384]{1,0:T(8,128)(2,1)S(1)}, u32[]{:S(2)}, u32[]{:S(2)}) collective-permute-start(bf16[192,384]{1,0:T(8,128)(2,1)S(1)} %bitcast.12), channel_id=1, source_target_pairs={{0,64},{64,128},{128,192},{192,0},{1,65},{65,129},{129,193},{193,1... | collective-permute-start | bytes 442376 | tf_op jit(solution)/shard_map/ppermute | solution.py:32
  34.2 0.1 turned_of.1.line
  34.3 2.1 %collective-permute-done.3.b0 = bf16[192,384]{1,0:T(8,128)(2,1)S(1)} collective-permute-done((bf16[192,384]{1,0:T(8,128)(2,1)S(1)}, bf16[192,384]{1,0:T(8,128)(2,1)S(1)}, u32[]{:S(2)}, u32[]{:S(2)}) %collective-permute-start.3) | collective-permute-done | bytes 147488 | tf_op jit(solution)/shard_map/ppermute | solution.py:32
  36.4 0.0 collective-permute-start.7
  36.4 0.0 collective-permute-done.6.a1
  36.4 3.4 %collective-permute-start.8 = (bf16[192,384]{1,0:T(8,128)(2,1)S(1)}, bf16[192,384]{1,0:T(8,128)(2,1)S(1)}, u32[]{:S(2)}, u32[]{:S(2)}) collective-permute-start(bf16[192,384]{1,0:T(8,128)(2,1)S(1)} %collective-permute-done.6.a1), channel_id=1, source_target_pairs={{0,192},{64,0},{128,64},{192,128},{1,193},{65,1},{129,65},{193,129... | collective-permute-start | bytes 442376 | tf_op jit(solution)/shard_map/ppermute | solution.py:32
  39.8 0.0 collective-permute-done.4.b1
  39.8 0.0 collective-permute-done.1.c1
  39.8 0.0 collective-permute-done.2.c3
  39.8 3.9 %shard_map.50 = (f32[4096,768]{1,0:T(8,128)S(1)}, f32[32,768]{1,0:T(8,128)S(1)}, f32[32,768]{1,0:T(8,128)S(1)}) custom-call(bf16[192,384]{1,0:T(8,128)(2,1)S(1)} %collective-permute-done.3.b0, bf16[192,384]{1,0:T(8,128)(2,1)S(1)} %collective-permute-done.4.b1, bf16[192,384]{1,0:T(8,128)(2,1)S(1)} %collective-permute-done.5.a0, ...), custom_call_target="tpu_custom_call" | custom-call | flops 2415919104 | bytes 12582912 | tf_op jit(solution)/shard_map/pallas_call | solution.py:191
  43.7 1.7 %shard_map.49 = (f32[4096,256]{1,0:T(8,128)S(1)}, f32[16,256]{1,0:T(8,128)S(1)}, f32[16,256]{1,0:T(8,128)S(1)}) custom-call(bf16[384,256]{1,0:T(8,128)(2,1)S(1)} %turned_of.1.line, bf16[1024,384]{1,0:T(8,128)(2,1)} %c0.5, bf16[1024,384]{1,0:T(8,128)(2,1)S(1)} %collective-permute-done.1.c1, bf16[1024,384]{1,0:T(8,128)(2,1)S(1)} %collective-permute-done.c2, ...), custom_call_target="tpu_custom_call" | custom-call | flops 805306368 | bytes 4194304 | tf_op jit(solution)/shard_map/pallas_call | solution.py:191
  45.4 0.0 collective-permute-done.7.f0
  45.4 0.0 collective-permute-done.8.f1
  45.4 2.9 %shard_map.51 = (f32[4096,512]{1,0:T(8,128)S(1)}, f32[32,512]{1,0:T(8,128)S(1)}, f32[384,128]{1,0:T(8,128)S(1)}) custom-call(bf16[192,384]{1,0:T(8,128)(2,1)S(1)} %collective-permute-done.7.f0, bf16[192,384]{1,0:T(8,128)(2,1)S(1)} %collective-permute-done.8.f1, bf16[384,384]{1,0:T(8,128)(2,1)S(1)} %bitcast.8, bf16[1024,384]{1,0:T(8,128)(2,1)} %c0.5, ...), custom_call_target="tpu_custom_call" | custom-call | flops 1610612736 | bytes 8388608 | tf_op jit(solution)/shard_map/pallas_call | solution.py:191
  48.3 13.9 %all_to_all.20 = f32[32,1,1536]{2,1,0:T(1,128)S(1)} all-to-all(f32[32,1,1536]{2,1,0:T(1,128)S(1)} %bitcast.10), channel_id=1, replica_groups=mesh['x'=4,'z'=8,'yh'=2,'core'=2,'rep'=2] {'x','z'}, dimensions={0} | all-to-all | bytes 393216 | tf_op jit(solution)/shard_map/all_to_all | solution.py:22
  62.2 2.3 %usage_of.1 = (f32[1,48]{1,0:T(1,128)}, f32[8,32,128]{2,1,0:T(8,128)S(1)}) custom-call(f32[4096,256]{1,0:T(8,128)S(1)} %get-tuple-element.20.own_probs, f32[16,256]{1,0:T(8,128)S(1)} %get-tuple-element.21.own_high, f32[4096,768]{1,0:T(8,128)S(1)} %get-tuple-element.22.near_probs, f32[32,768]{1,0:T(8,128)S(1)} %get-tuple-element.23.near_high, ...), custom_call_target="tpu_custom_call" | custom-call | flops 12582912 | bytes 25165824 | tf_op jit(solution)/shard_map/usage_of/pallas_call | solution.py:284
  64.4 14.4 %all_to_all.21.counts = f32[8,32,128]{2,1,0:T(8,128)S(1)} all-to-all(f32[8,32,128]{2,1,0:T(8,128)S(1)} %get-tuple-element.30), channel_id=1, replica_groups=mesh['x'=4,'z'=8,'yh'=2,'core'=2,'rep'=2] {'yh','core','rep'}, dimensions={0} | all-to-all | bytes 262144 | tf_op jit(solution)/shard_map/all_to_all | solution.py:22
  78.8 0.6 entropy_of.1
  79.4 12.5 %all_to_all.22 = f32[32,1,128]{2,1,0:T(1,128)S(1)} all-to-all(f32[32,1,128]{2,1,0:T(1,128)S(1)} %get-tuple-element.32), channel_id=1, replica_groups=mesh['x'=4,'z'=8,'yh'=2,'core'=2,'rep'=2] {'x','z'}, dimensions={0} | all-to-all | bytes 32768 | tf_op jit(solution)/shard_map/all_to_all | solution.py:22
  91.9 0.6 slice_reduce_fusion
  (1 shorter events, 0.0 us)
Async XLA Ops:
  0.6 24.1 %collective-permute-start = (bf16[1024,384]{1,0:T(8,128)(2,1)}, bf16[1024,384]{1,0:T(8,128)(2,1)S(1)}, u32[]{:S(2)}, u32[]{:S(2)}) collective-permute-start(bf16[1024,384]{1,0:T(8,128)(2,1)} %c0.5), channel_id=1, source_target_pairs={{0,5},{5,0},{1,4},{4,1},{2,7},{7,2},{3,6},{6,3},{8,13},{13,8},{9,1... | collective-permute-start | bytes 2359304 | tf_op jit(solution)/shard_map/ppermute | solution.py:345
  5.8 19.0 %all-to-all-start = ((bf16[8,48,384]{2,1,0:T(8,128)(2,1)}), bf16[8,48,384]{2,1,0:T(8,128)(2,1)S(1)}, u32[]{:S(2)}, u32[]{:S(2)}) async-start(bf16[8,48,384]{2,1,0:T(8,128)(2,1)} %broadcast_in_dim.3), calls=%async_computation | async-start | bytes 589824 | tf_op jit(solution)/shard_map/all_to_all | solution.py:22
  14.0 25.8 %collective-permute-start.1 = (bf16[1024,384]{1,0:T(8,128)(2,1)}, bf16[1024,384]{1,0:T(8,128)(2,1)S(1)}, u32[]{:S(2)}, u32[]{:S(2)}) collective-permute-start(bf16[1024,384]{1,0:T(8,128)(2,1)} %c0.5), channel_id=1, source_target_pairs={{0,2},{2,0},{1,3},{3,1},{4,6},{6,4},{5,7},{7,5},{8,10},{10,8},{9,1... | collective-permute-start | bytes 2359304 | tf_op jit(solution)/shard_map/ppermute | solution.py:346
  24.7 15.0 %collective-permute-start.2 = (bf16[1024,384]{1,0:T(8,128)(2,1)S(1)}, bf16[1024,384]{1,0:T(8,128)(2,1)S(1)}, u32[]{:S(2)}, u32[]{:S(2)}) collective-permute-start(bf16[1024,384]{1,0:T(8,128)(2,1)S(1)} %collective-permute-done.c2), channel_id=1, source_target_pairs={{0,2},{2,0},{1,3},{3,1},{4,6},{6,4},{5,7},{7,5},{8,10},{10,8},{9,1... | collective-permute-start | bytes 2359304 | tf_op jit(solution)/shard_map/ppermute | solution.py:355
  27.5 5.8 %collective-permute-start.5 = (bf16[192,384]{1,0:T(8,128)(2,1)S(1)}, bf16[192,384]{1,0:T(8,128)(2,1)S(1)}, u32[]{:S(2)}, u32[]{:S(2)}) collective-permute-start(bf16[192,384]{1,0:T(8,128)(2,1)S(1)} %bitcast.13), channel_id=1, source_target_pairs={{0,192},{64,0},{128,64},{192,128},{1,193},{65,1},{129,65},{193,129... | collective-permute-start | bytes 442376 | tf_op jit(solution)/shard_map/ppermute | solution.py:32
  30.1 6.3 %collective-permute-start.3 = (bf16[192,384]{1,0:T(8,128)(2,1)S(1)}, bf16[192,384]{1,0:T(8,128)(2,1)S(1)}, u32[]{:S(2)}, u32[]{:S(2)}) collective-permute-start(bf16[192,384]{1,0:T(8,128)(2,1)S(1)} %bitcast.14), channel_id=1, source_target_pairs={{0,64},{64,128},{128,192},{192,0},{1,65},{65,129},{129,193},{193,1... | collective-permute-start | bytes 442376 | tf_op jit(solution)/shard_map/ppermute | solution.py:32
  30.1 6.3 %collective-permute-start.6 = (bf16[192,384]{1,0:T(8,128)(2,1)S(1)}, bf16[192,384]{1,0:T(8,128)(2,1)S(1)}, u32[]{:S(2)}, u32[]{:S(2)}) collective-permute-start(bf16[192,384]{1,0:T(8,128)(2,1)S(1)} %bitcast.11), channel_id=1, source_target_pairs={{0,192},{64,0},{128,64},{192,128},{1,193},{65,1},{129,65},{193,129... | collective-permute-start | bytes 442376 | tf_op jit(solution)/shard_map/ppermute | solution.py:32
  33.3 6.5 %collective-permute-start.4 = (bf16[192,384]{1,0:T(8,128)(2,1)S(1)}, bf16[192,384]{1,0:T(8,128)(2,1)S(1)}, u32[]{:S(2)}, u32[]{:S(2)}) collective-permute-start(bf16[192,384]{1,0:T(8,128)(2,1)S(1)} %bitcast.12), channel_id=1, source_target_pairs={{0,64},{64,128},{128,192},{192,0},{1,65},{65,129},{129,193},{193,1... | collective-permute-start | bytes 442376 | tf_op jit(solution)/shard_map/ppermute | solution.py:32
  36.4 9.0 %collective-permute-start.7 = (bf16[192,384]{1,0:T(8,128)(2,1)S(1)}, bf16[192,384]{1,0:T(8,128)(2,1)S(1)}, u32[]{:S(2)}, u32[]{:S(2)}) collective-permute-start(bf16[192,384]{1,0:T(8,128)(2,1)S(1)} %collective-permute-done.3.b0), channel_id=1, source_target_pairs={{0,64},{64,128},{128,192},{192,0},{1,65},{65,129},{129,193},{193,1... | collective-permute-start | bytes 442376 | tf_op jit(solution)/shard_map/ppermute | solution.py:32
  36.4 9.0 %collective-permute-start.8 = (bf16[192,384]{1,0:T(8,128)(2,1)S(1)}, bf16[192,384]{1,0:T(8,128)(2,1)S(1)}, u32[]{:S(2)}, u32[]{:S(2)}) collective-permute-start(bf16[192,384]{1,0:T(8,128)(2,1)S(1)} %collective-permute-done.6.a1), channel_id=1, source_target_pairs={{0,192},{64,0},{128,64},{192,128},{1,193},{65,1},{129,65},{193,129... | collective-permute-start | bytes 442376 | tf_op jit(solution)/shard_map/ppermute | solution.py:32
